TPU v7x, 8 devices: a whole 2x2x1 slice. The times are simulated.
8 devices in a mesh: ep: 2 (over z, y), dp: 4 (over x, core).
Axes of the slice: x: 2, y: 2, z: 1, core: 2. Of those that a mesh axis runs over, the one named last changes fastest.
Arguments:
- tokens: bfloat16 [8192, 448], P(('dp', 'ep'))
- d_out: bfloat16 [8192, 448], P(('dp', 'ep'))
- expert_ids: int32 [2, 8192, 8], P(None, ('dp', 'ep'))
- gate_vals: float32 [2, 8192, 8], P(None, ('dp', 'ep'))
- w_mix: bfloat16 [2, 448, 448], replicated
- w_gate: bfloat16 [2, 64, 448, 320], P(None, 'ep')
- w_up: bfloat16 [2, 64, 448, 320], P(None, 'ep')
- w_down: bfloat16 [2, 64, 320, 448], P(None, 'ep')
Outputs:
- output 1: bfloat16 [8192, 448], P(('dp', 'ep'))
- output 2: bfloat16 [8192, 448], P(('dp', 'ep'))
- output 3: bfloat16 [2, 448, 448], replicated
- output 4: bfloat16 [2, 64, 448, 320], P(None, 'ep')
- output 5: bfloat16 [2, 64, 448, 320], P(None, 'ep')
- output 6: bfloat16 [2, 64, 320, 448], P(None, 'ep')
All inputs are finite; a program needn't handle non-finite values.
Results may differ from a plain program's by a relative error of at most 0.0171451.
Values are sent between devices in bfloat16 or wider.
A program may use at most 1 GiB of HBM per device.

v0:
```python
import jax
import jax.numpy as jnp
from jax import lax
from jax.sharding import PartitionSpec as P

CAP_FACTOR = 3


def silu_parts(pre_gate):
    sig_val = jax.nn.sigmoid(pre_gate)
    return pre_gate * sig_val, sig_val * (1.0 + pre_gate * (1.0 - sig_val))


def route_tables(expert_ids, n_experts, capacity):
    flat_ids = expert_ids.reshape(-1)
    n_copies = flat_ids.shape[0]
    sort_order = jnp.argsort(flat_ids, stable=True)
    counts = jnp.bincount(flat_ids, length=n_experts)
    starts = jnp.cumsum(counts) - counts
    slot_pos = jnp.arange(capacity)
    src_copy = sort_order[jnp.minimum(starts[:, None] + slot_pos[None, :], n_copies - 1)]
    is_valid = slot_pos[None, :] < counts[:, None]
    sorted_ids = flat_ids[sort_order]
    rows_sorted = sorted_ids * capacity + jnp.arange(n_copies) - starts[sorted_ids]
    copy_row = jnp.zeros_like(flat_ids).at[sort_order].set(rows_sorted)
    return src_copy, is_valid, copy_row


def layer_forward(x_in, expert_ids, gate_vals, w_mix, w_gate, w_up, w_down, n_experts, capacity):
    tok_local, d_model = x_in.shape
    top_k = expert_ids.shape[1]
    n_local = w_gate.shape[0]
    mixed = x_in.astype(jnp.float32) + jnp.dot(x_in, w_mix, preferred_element_type=jnp.float32)
    u_act = mixed.astype(jnp.bfloat16)
    src_copy, is_valid, copy_row = route_tables(expert_ids, n_experts, capacity)
    send_buf = jnp.where(is_valid[:, :, None], u_act[src_copy // top_k], 0)
    send_buf = send_buf.reshape(n_experts // n_local, n_local, capacity, d_model)
    recv_buf = lax.all_to_all(send_buf, 'ep', 0, 0, tiled=True)
    pre_gate = jnp.einsum('secd,edf->secf', recv_buf, w_gate, preferred_element_type=jnp.float32)
    pre_up = jnp.einsum('secd,edf->secf', recv_buf, w_up, preferred_element_type=jnp.float32)
    act, _ = silu_parts(pre_gate)
    hidden = (act * pre_up).astype(jnp.bfloat16)
    out_buf = jnp.einsum('secf,efd->secd', hidden, w_down, preferred_element_type=jnp.float32).astype(jnp.bfloat16)
    back_buf = lax.all_to_all(out_buf, 'ep', 0, 0, tiled=True).reshape(n_experts * capacity, d_model)
    out_copy = back_buf[copy_row].reshape(tok_local, top_k, d_model)
    y_out = u_act.astype(jnp.float32) + jnp.sum(gate_vals[:, :, None] * out_copy.astype(jnp.float32), axis=1)
    saved = (x_in, src_copy, is_valid, copy_row, recv_buf, pre_gate, pre_up, hidden)
    return y_out.astype(jnp.bfloat16), saved


def layer_backward(saved, d_y, gate_vals, w_mix, w_gate, w_up, w_down):
    x_in, src_copy, is_valid, copy_row, recv_buf, pre_gate, pre_up, hidden = saved
    tok_local, d_model = d_y.shape
    top_k = gate_vals.shape[1]
    n_experts, capacity = is_valid.shape
    g_dy = (gate_vals[:, :, None] * d_y.astype(jnp.float32)[:, None, :]).astype(jnp.bfloat16)
    g_dy = g_dy.reshape(tok_local * top_k, d_model)
    send_grad = jnp.where(is_valid[:, :, None], g_dy[src_copy], 0).reshape(recv_buf.shape)
    recv_grad = lax.all_to_all(send_grad, 'ep', 0, 0, tiled=True)
    d_hidden = jnp.einsum('secd,efd->secf', recv_grad, w_down, preferred_element_type=jnp.float32)
    act, act_slope = silu_parts(pre_gate)
    d_pre_gate = (d_hidden * pre_up * act_slope).astype(jnp.bfloat16)
    d_pre_up = (d_hidden * act).astype(jnp.bfloat16)
    d_recv = (jnp.einsum('secf,edf->secd', d_pre_gate, w_gate, preferred_element_type=jnp.float32)
              + jnp.einsum('secf,edf->secd', d_pre_up, w_up, preferred_element_type=jnp.float32)).astype(jnp.bfloat16)
    g_gate = jnp.einsum('secd,secf->edf', recv_buf, d_pre_gate, preferred_element_type=jnp.float32).astype(jnp.bfloat16)
    g_up = jnp.einsum('secd,secf->edf', recv_buf, d_pre_up, preferred_element_type=jnp.float32).astype(jnp.bfloat16)
    g_down = jnp.einsum('secf,secd->efd', hidden, recv_grad, preferred_element_type=jnp.float32).astype(jnp.bfloat16)
    g_gate = lax.psum(g_gate, 'dp')
    g_up = lax.psum(g_up, 'dp')
    g_down = lax.psum(g_down, 'dp')
    d_back = lax.all_to_all(d_recv, 'ep', 0, 0, tiled=True).reshape(n_experts * capacity, d_model)
    d_copy = d_back[copy_row].reshape(tok_local, top_k, d_model)
    d_u = (d_y.astype(jnp.float32)
           + jnp.sum(gate_vals[:, :, None] * d_copy.astype(jnp.float32), axis=1)).astype(jnp.bfloat16)
    g_mix = jnp.einsum('td,te->de', x_in, d_u, preferred_element_type=jnp.float32).astype(jnp.bfloat16)
    g_mix = lax.psum(g_mix, ('dp', 'ep'))
    d_x = (d_u.astype(jnp.float32)
           + jnp.einsum('te,de->td', d_u, w_mix, preferred_element_type=jnp.float32)).astype(jnp.bfloat16)
    return d_x, (g_mix, g_gate, g_up, g_down)


def stack_part(grads, index):
    return jnp.stack([entry[index] for entry in grads])


def solution(mesh):
    ep_size = mesh.shape['ep']
    tok_spec = P(('dp', 'ep'), None)
    route_spec = P(None, ('dp', 'ep'), None)
    whole_spec = P(None, None, None)
    expert_spec = P(None, 'ep', None, None)

    def device_step(tokens, d_out, expert_ids, gate_vals, w_mix, w_gate, w_up, w_down):
        n_layers = w_mix.shape[0]
        n_experts = w_gate.shape[1] * ep_size
        tok_local = tokens.shape[0]
        top_k = expert_ids.shape[2]
        capacity = (CAP_FACTOR * tok_local * top_k + n_experts - 1) // n_experts
        layer_in = tokens
        saved_all = []
        for layer in range(n_layers):
            layer_in, saved = layer_forward(layer_in, expert_ids[layer], gate_vals[layer], w_mix[layer],
                                            w_gate[layer], w_up[layer], w_down[layer], n_experts, capacity)
            saved_all.append(saved)
        d_y = d_out
        grads = []
        for layer in reversed(range(n_layers)):
            d_y, grad_set = layer_backward(saved_all[layer], d_y, gate_vals[layer], w_mix[layer],
                                           w_gate[layer], w_up[layer], w_down[layer])
            grads.insert(0, grad_set)
        return (layer_in, d_y, stack_part(grads, 0), stack_part(grads, 1),
                stack_part(grads, 2), stack_part(grads, 3))

    return jax.shard_map(device_step, mesh=mesh,
                         in_specs=(tok_spec, tok_spec, route_spec, route_spec, whole_spec,
                                   expert_spec, expert_spec, expert_spec),
                         out_specs=(tok_spec, tok_spec, whole_spec, expert_spec, expert_spec, expert_spec),
                         check_vma=False)
```

profile of v0, /device:TPU:0, one launch (start us, length us, event | category | flops | bytes accessed | tf_op | source)
XLA Modules:
  0.0 4757.5 jit_solution(3842210597793256295)
XLA Ops:
  9.1 57.0 %scatter_custom_fusion = s32[64]{0:T(128)S(1)} fusion(s32[8192]{0:T(1024)S(1)} %reshape.686, s32[8192]{0:T(1024)S(1)} %broadcast.633, s32[]{:T(128)} %constant.39.clone.1), kind=kCustom, calls=%fused_computation.329 | custom fusion | flops 8192 | bytes 260 | tf_op jit(solution)/shard_map/scatter-add | solution.py:18
  74.5 135.5 %gather_fusion = s32[24576]{0:T(1024)S(1)} fusion(s32[8192]{0:T(1024)S(1)} %get-tuple-element.8, s32[24576]{0:T(1024)S(1)} %broadcast_clamp_fusion.5), kind=kCustom, calls=%fused_computation | custom fusion | bytes 294912 | tf_op jit(solution)/shard_map/gather | solution.py:21
  213.1 99.2 %gather_fusion.1 = bf16[24576,448]{1,0:T(8,128)(2,1)} fusion(bf16[1024,448]{1,0:T(8,128)(2,1)S(1)} %copy.64, s32[24576]{0:T(1024)S(1)} %broadcast_clamp_fusion.1), kind=kCustom, calls=%fused_computation.1 | custom fusion | bytes 44138496 | tf_op jit(solution)/shard_map/gather | solution.py:36
  355.0 54.1 %copy.66 = bf16[2,32,384,448]{2,3,1,0:T(8,128)(2,1)S(1)} copy(bf16[2,32,384,448]{2,1,0,3:T(8,128)(2,1)S(1)} %broadcast_select_fusion.3) | data formatting | bytes 44040192 | tf_op jit(solution)/shard_map/jit(_where)/select_n | solution.py:36
  409.1 246.8 %all_to_all.40 = bf16[2,32,384,448]{2,3,1,0:T(8,128)(2,1)} all-to-all(bf16[2,32,384,448]{2,3,1,0:T(8,128)(2,1)S(1)} %copy.66), channel_id=1, replica_groups=mesh['ep'=2,'dp'=4] {'ep'}, dimensions={0} | all-to-all | bytes 44040192 | tf_op jit(solution)/shard_map/all_to_all | solution.py:38
  777.0 57.2 %scatter_custom_fusion.2 = s32[64]{0:T(128)S(1)} fusion(s32[8192]{0:T(1024)S(1)} %reshape.702, s32[8192]{0:T(1024)} %copy-done.36, s32[]{:T(128)} %constant.39.clone.1), kind=kCustom, calls=%fused_computation.327 | custom fusion | flops 8192 | bytes 768 | tf_op jit(solution)/shard_map/scatter-add | solution.py:18
  842.6 135.9 %gather_fusion.4 = s32[24576]{0:T(1024)S(1)} fusion(s32[8192]{0:T(1024)S(1)} %get-tuple-element.9, s32[24576]{0:T(1024)S(1)} %broadcast_clamp_fusion.4), kind=kCustom, calls=%fused_computation.4 | custom fusion | bytes 294912 | tf_op jit(solution)/shard_map/gather | solution.py:21
  979.3 45.5 gather_fusion.2
  1029.5 104.1 %gather_fusion.8 = bf16[24576,448]{1,0:T(8,128)(2,1)} fusion(bf16[8192,448]{1,0:T(8,128)(2,1)} %fusion.41, s32[24576]{0:T(1024)S(1)} %broadcast_clamp_fusion.3), kind=kCustom, calls=%fused_computation.8 | custom fusion | bytes 44138496 | tf_op jit(solution)/shard_map/gather | solution.py:58
  1275.1 45.4 gather_fusion.3
  1333.7 106.9 %gather_fusion.5 = bf16[24576,448]{1,0:T(8,128)(2,1)} fusion(bf16[1024,448]{1,0:T(8,128)(2,1)S(1)} %copy.77, s32[24576]{0:T(1024)} %broadcast_clamp_fusion), kind=kCustom, calls=%fused_computation.5 | custom fusion | bytes 44138496 | tf_op jit(solution)/shard_map/gather | solution.py:36
  1558.0 215.3 %all-to-all-done.4 = bf16[2,32,384,448]{2,3,1,0:T(8,128)(2,1)} async-done(((bf16[2,32,384,448]{2,3,1,0:T(8,128)(2,1)}), bf16[2,32,384,448]{2,3,1,0:T(8,128)(2,1)}, u32[]{:S(2)}, u32[]{:S(2)}) %all-to-all-start.4) | async-done | bytes 22020128 | tf_op jit(solution)/shard_map/all_to_all | solution.py:59
  1809.7 212.0 %all-to-all-done.2 = bf16[2,32,384,448]{2,3,1,0:T(8,128)(2,1)} async-done(((bf16[2,32,384,448]{2,3,1,0:T(8,128)(2,1)}), bf16[2,32,384,448]{2,3,1,0:T(8,128)(2,1)}, u32[]{:S(2)}, u32[]{:S(2)}) %all-to-all-start.2) | async-done | bytes 22020128 | tf_op jit(solution)/shard_map/all_to_all | solution.py:38
  2046.6 47.9 %fusion.6 = (bf16[2,32,384,320]{2,3,0,1:T(8,128)(2,1)}, bf16[2,32,384,320]{2,3,0,1:T(8,128)(2,1)}, bf16[2,32,384,320]{2,3,0,1:T(8,128)(2,1)}) fusion(f32[32,2,384,320]{2,3,1,0:T(8,128)} %fusion.28, f32[32,2,384,320]{2,3,1,0:T(8,128)} %fusion.26, bf16[2,32,384,448]{2,3,1,0:T(8,128)(2,1)} %all-to-all-done.2, bf16[2,32,448,320]{2,3,1,0:T(8,128)(2,1)} %param.14), kind=kOutput, calls=%fused_computation.29 | convolution fusion | flops 7164395520 | bytes 142606336 | tf_op jit(solution)/shard_map/secd,edf->secf/dot_general | solution.py:40
  2230.6 155.5 %all-to-all-done.3 = bf16[2,32,384,448]{2,3,1,0:T(8,128)(2,1)} async-done(((bf16[2,32,384,448]{2,3,1,0:T(8,128)(2,1)}), bf16[2,32,384,448]{2,3,1,0:T(8,128)(2,1)}, u32[]{:S(2)}, u32[]{:S(2)}) %all-to-all-start.3) | async-done | bytes 22020128 | tf_op jit(solution)/shard_map/all_to_all | solution.py:44
  2398.6 45.7 gather_fusion.6
  2553.9 45.3 gather_fusion.7
  2661.8 45.4 gather_fusion.9
  2734.4 104.3 %gather_fusion.10 = bf16[24576,448]{1,0:T(8,128)(2,1)} fusion(bf16[8192,448]{1,0:T(8,128)(2,1)} %fusion.40, s32[24576]{0:T(1024)S(1)} %copy-done.24), kind=kCustom, calls=%fused_computation.10 | custom fusion | bytes 44138496 | tf_op jit(solution)/shard_map/gather | solution.py:58
  2881.5 54.1 %copy.98 = bf16[2,32,384,448]{2,3,1,0:T(8,128)(2,1)S(1)} copy(bf16[2,32,384,448]{2,1,0,3:T(8,128)(2,1)S(1)} %broadcast_select_fusion.2) | data formatting | bytes 44040192 | tf_op jit(solution)/shard_map/jit(_where)/select_n | solution.py:58
  2935.6 241.6 %all_to_all.41 = bf16[2,32,384,448]{2,3,1,0:T(8,128)(2,1)} all-to-all(bf16[2,32,384,448]{2,3,1,0:T(8,128)(2,1)S(1)} %copy.98), channel_id=1, replica_groups=mesh['ep'=2,'dp'=4] {'ep'}, dimensions={0} | all-to-all | bytes 44040192 | tf_op jit(solution)/shard_map/all_to_all | solution.py:59
  3408.3 136.5 %all-to-all-done.7 = bf16[2,32,384,448]{2,3,1,0:T(8,128)(2,1)} async-done(((bf16[2,32,384,448]{2,3,1,0:T(8,128)(2,1)}), bf16[2,32,384,448]{2,3,1,0:T(8,128)(2,1)}, u32[]{:S(2)}, u32[]{:S(2)}) %all-to-all-start.7) | async-done | bytes 22020128 | tf_op jit(solution)/shard_map/all_to_all | solution.py:72
  3573.9 45.4 gather_fusion.11
  3679.9 1024.7 %all-reduce.7.cloned.1.call-done = (bf16[1,32,448,320]{2,3,1,0:T(8,128)(2,1)}, bf16[1,32,448,320]{2,3,1,0:T(8,128)(2,1)}, bf16[1,32,448,320]{2,3,1,0:T(8,128)(2,...) async-done(((bf16[1,32,448,320]{2,3,1,0:T(8,128)(2,1)}, bf16[1,32,448,320]{2,3,1,0:T(8,128)(2,1)}, ...) | async-done | bytes 55050256 | tf_op jit(solution)/shard_map/psum | solution.py:69
  (221 shorter events, 1281.0 us)
Async XLA Ops:
  9.0 58.1 %copy-start.36 = (s32[8192]{0:T(1024)}, s32[8192]{0:T(1024)S(1)}, u32[]{:S(2)}) copy-start(s32[8192]{0:T(1024)S(1)} %broadcast.633) | copy-start | bytes 98308
  66.2 277.6 %copy-start.28 = (pred[2,32,384]{2,1,0:T(8,128)(4,1)}, pred[2,32,384]{2,1,0:T(8,128)(4,1)S(1)}, u32[]{:S(2)}) copy-start(pred[2,32,384]{2,1,0:T(8,128)(4,1)S(1)} %iota_compare_fusion.1) | copy-start | bytes 73732
  67.7 142.3 %copy-start.6 = (s32[8192]{0:T(1024)}, s32[8192]{0:T(1024)S(1)}, u32[]{:S(2)}) copy-start(s32[8192]{0:T(1024)S(1)} %reshape_squeeze.6) | copy-start | bytes 98308
  74.5 135.6 %copy-start.2 = (s32[8192]{0:T(1024)}, s32[8192]{0:T(1024)S(1)}, u32[]{:S(2)}) copy-start(s32[8192]{0:T(1024)S(1)} %get-tuple-element.8) | copy-start | bytes 98308
  74.5 136.3 %copy-start.37 = (bf16[1024,448]{0,1:T(8,128)(2,1)S(1)}, bf16[1024,448]{0,1:T(8,128)(2,1)}, u32[]{:S(2)}) copy-start(bf16[1024,448]{0,1:T(8,128)(2,1)} %param.8) | copy-start | bytes 2752516
  212.5 99.7 %copy-start.17 = (bf16[1024,448]{0,1:T(8,128)(2,1)}, bf16[1024,448]{0,1:T(8,128)(2,1)S(1)}, u32[]{:S(2)}) copy-start(bf16[1024,448]{0,1:T(8,128)(2,1)S(1)} %add_convert_fusion.9) | copy-start | bytes 2752516
  763.1 72.2 %copy-start.32 = (s32[1,1024,8]{1,2,0:T(8,128)S(1)}, s32[1,1024,8]{1,2,0:T(8,128)}, u32[]{:S(2)}) copy-start(s32[1,1024,8]{1,2,0:T(8,128)} %get-tuple-element.171) | copy-start | bytes 98308
  763.1 483.1 %all-to-all-start.1 = ((bf16[2,32,384,448]{2,3,1,0:T(8,128)(2,1)}), bf16[2,32,384,448]{2,3,1,0:T(8,128)(2,1)}, u32[]{:S(2)}, u32[]{:S(2)}) async-start(bf16[2,32,384,448]{2,3,1,0:T(8,128)(2,1)} %copy.69), calls=%async_computation.1 | async-start | bytes 44040192 | tf_op jit(solution)/shard_map/all_to_all | solution.py:44
  842.6 136.0 %copy-start = (s32[8192]{0:T(1024)}, s32[8192]{0:T(1024)S(1)}, u32[]{:S(2)}) copy-start(s32[8192]{0:T(1024)S(1)} %get-tuple-element.9) | copy-start | bytes 98308
  842.6 136.1 %copy-start.3 = (s32[8192]{0:T(1024)S(1)}, s32[8192]{0:T(1024)}, u32[]{:S(2)}) copy-start(s32[8192]{0:T(1024)} %copy-done.2) | copy-start | bytes 98308
  1333.2 107.4 %copy-start.12 = (bf16[1024,448]{0,1:T(8,128)(2,1)}, bf16[1024,448]{0,1:T(8,128)(2,1)S(1)}, u32[]{:S(2)}) copy-start(bf16[1024,448]{0,1:T(8,128)(2,1)S(1)} %add_convert_fusion.7) | copy-start | bytes 2752516
  1523.9 249.3 %all-to-all-start.4 = ((bf16[2,32,384,448]{2,3,1,0:T(8,128)(2,1)}), bf16[2,32,384,448]{2,3,1,0:T(8,128)(2,1)}, u32[]{:S(2)}, u32[]{:S(2)}) async-start(bf16[2,32,384,448]{2,3,1,0:T(8,128)(2,1)} %copy.89), calls=%async_computation.4 | async-start | bytes 44040192 | tf_op jit(solution)/shard_map/all_to_all | solution.py:59
  1773.2 248.5 %all-to-all-start.2 = ((bf16[2,32,384,448]{2,3,1,0:T(8,128)(2,1)}), bf16[2,32,384,448]{2,3,1,0:T(8,128)(2,1)}, u32[]{:S(2)}, u32[]{:S(2)}) async-start(bf16[2,32,384,448]{2,3,1,0:T(8,128)(2,1)} %copy.79), calls=%async_computation.2 | async-start | bytes 44040192 | tf_op jit(solution)/shard_map/all_to_all | solution.py:38
  2138.0 248.1 %all-to-all-start.3 = ((bf16[2,32,384,448]{2,3,1,0:T(8,128)(2,1)}), bf16[2,32,384,448]{2,3,1,0:T(8,128)(2,1)}, u32[]{:S(2)}, u32[]{:S(2)}) async-start(bf16[2,32,384,448]{2,3,1,0:T(8,128)(2,1)} %copy.82), calls=%async_computation.3 | async-start | bytes 44040192 | tf_op jit(solution)/shard_map/all_to_all | solution.py:44
  2230.6 166.8 %copy-start.31 = (f32[1,1024,8]{1,2,0:T(8,128)S(1)}, f32[1,1024,8]{1,2,0:T(8,128)}, u32[]{:S(2)}) copy-start(f32[1,1024,8]{1,2,0:T(8,128)} %get-tuple-element.165) | copy-start | bytes 98308
  2230.6 167.8 %copy-start.30 = (f32[1024,8]{0,1:T(8,128)S(1)}, f32[1024,8]{0,1:T(8,128)}, u32[]{:S(2)}) copy-start(f32[1024,8]{0,1:T(8,128)} %get-tuple-element.167) | copy-start | bytes 98308
  2230.6 168.0 %copy-start.1 = (s32[8192]{0:T(1024)S(1)}, s32[8192]{0:T(1024)}, u32[]{:S(2)}) copy-start(s32[8192]{0:T(1024)} %copy-done) | copy-start | bytes 98308
  2230.6 168.1 %copy-start.5 = (s32[8192]{0:T(1024)S(1)}, s32[8192]{0:T(1024)}, u32[]{:S(2)}) copy-start(s32[8192]{0:T(1024)} %copy-done.4) | copy-start | bytes 98308
  2386.1 246.9 %all-to-all-start.5 = ((bf16[2,32,384,448]{2,3,1,0:T(8,128)(2,1)}), bf16[2,32,384,448]{2,3,1,0:T(8,128)(2,1)}, u32[]{:S(2)}, u32[]{:S(2)}) async-start(bf16[2,32,384,448]{2,3,1,0:T(8,128)(2,1)} %copy.91), calls=%async_computation.5 | async-start | bytes 44040192 | tf_op jit(solution)/shard_map/all_to_all | solution.py:72
  3299.4 245.5 %all-to-all-start.7 = ((bf16[2,32,384,448]{2,3,1,0:T(8,128)(2,1)}), bf16[2,32,384,448]{2,3,1,0:T(8,128)(2,1)}, u32[]{:S(2)}, u32[]{:S(2)}) async-start(bf16[2,32,384,448]{2,3,1,0:T(8,128)(2,1)} %copy.100), calls=%async_computation.7 | async-start | bytes 44040192 | tf_op jit(solution)/shard_map/all_to_all | solution.py:72
  3310.7 366.6 %all-reduce.5.cloned.1.call-start = ((), (), s32[]{:S(2)}) async-start(), calls=%async_computation.8 | async-start | bytes 1835008 | tf_op jit(solution)/shard_map/psum | solution.py:77
  3408.3 165.5 %copy-start.27 = (s32[8192]{0:T(1024)S(1)}, s32[8192]{0:T(1024)}, u32[]{:S(2)}) copy-start(s32[8192]{0:T(1024)} %copy-done.26) | copy-start | bytes 98308
  3573.9 58.4 %copy-start.38 = (bf16[1024,448]{0,1:T(8,128)(2,1)S(1)}, bf16[1024,448]{0,1:T(8,128)(2,1)}, u32[]{:S(2)}) copy-start(bf16[1024,448]{0,1:T(8,128)(2,1)} %param.8) | copy-start | bytes 2752516
  3633.8 1070.8 %all-reduce.7.cloned.1.call-start = ((), (), s32[]{:S(2)}) async-start(), calls=%async_computation.9 | async-start | bytes 125829120 | tf_op jit(solution)/shard_map/psum | solution.py:69
  (23 other events, 520.3 us)
Sparse Core Ops, SparseCore 0:
  3633.9 43.4 all-reduce.4
  3681.0 1023.4 all-reduce.6
where the time goes:
time: 4780 us; the launch traced here: 4760 us
  waiting for transfers between devices  1790 us (37%)
  local copies, waits for them, and re-layouts  1520 us (32%)
  matrix products  504 us (11%)
  blocking collectives  488 us (10%)
  other arithmetic  368 us (8%)
  starting transfers between devices  68.5 us (1%)
    psum x1, waiting for transfers between devices, layer_backward(): g_gate = lax.psum(g_gate, 'dp')  1020 us
    gather x4, local copies, waits for them, and re-layouts, layer_backward(): g_dy[src_copy]  272 us
    gather x4, local copies, waits for them, and re-layouts, route_tables(): sort_order[jnp.minimum(starts[:, None] + slot_pos[None, :], n_copies - 1)]  272 us
    gather x4, local copies, waits for them, and re-layouts, layer_forward(): send_buf = jnp.where(is_valid[:, :, None], u_act[src_copy // top_k], 0)  269 us
    all_to_all x1, blocking collectives, layer_forward(): recv_buf = lax.all_to_all(send_buf, 'ep', 0, 0, tiled=True)  247 us
    all_to_all x1, blocking collectives, layer_backward(): recv_grad = lax.all_to_all(send_grad, 'ep', 0, 0, tiled=True)  242 us
    all_to_all x1, waiting for transfers between devices, layer_backward(): recv_grad = lax.all_to_all(send_grad, 'ep', 0, 0, tiled=True)  215 us
    all_to_all x1, waiting for transfers between devices, layer_forward(): recv_buf = lax.all_to_all(send_buf, 'ep', 0, 0, tiled=True)  212 us
  transfers between devices with their start and end apart: 8, of which 7 were waited for; matrix products, arithmetic and copies ran while one was open for 19% of the time, Pallas kernels for 0%

commit v1 on v0

v1 whole, which is shorter than its diff:
```python
import functools

import jax
import jax.numpy as jnp
from jax import lax
from jax.experimental import pallas as pl
from jax.experimental.pallas import tpu as pltpu
from jax.sharding import Mesh, PartitionSpec as P

F32, BF16, I32 = jnp.float32, jnp.bfloat16, jnp.int32
ROWS = 384
GRP = 8
CAP_FACTOR = 3
LANES = 128
VMEM_LIMIT = 62 * 1024 * 1024


def cdiv(a, b):
    return (a + b - 1) // b


def local_lists(expert_ids, gate_vals, n_exp):
    n_layers, n_tok, top = expert_ids.shape
    n = n_tok * top
    flat = expert_ids.reshape(n_layers, n)
    gates = gate_vals.reshape(n_layers, n)
    step = 2 * n
    big = n_exp * step + n
    real = flat * step + jnp.arange(n, dtype=I32)[None]
    counts = jnp.sum((flat[:, :, None] == jnp.arange(n_exp, dtype=I32)).astype(I32), axis=1)
    pad = (-counts) % GRP
    k = jnp.arange(GRP - 1, dtype=I32)
    fill = jnp.where(k[None, None] < pad[:, :, None],
                     jnp.arange(n_exp, dtype=I32)[None, :, None] * step + n, big)
    tail = 128 - (n_exp * (GRP - 1)) % 128
    keys = jnp.concatenate([real, fill.reshape(n_layers, -1), jnp.full((n_layers, tail), big, I32)], 1)
    gts = jnp.pad(gates, ((0, 0), (0, keys.shape[1] - n)))
    keys, gts = lax.sort((keys, gts), dimension=1, num_keys=1)
    low = keys % step
    tok = jnp.where(low >= n, -1, low // top)
    return tok, gts, (counts + pad) // GRP


def half_tables(tok, gts, groups, experts, n_tok, max_groups):
    n_src, length = tok.shape
    dummy = n_src * n_tok
    idx = jnp.where(tok < 0, dummy, tok + jnp.arange(n_src, dtype=I32)[:, None] * n_tok) * 4
    starts = jnp.cumsum(groups, axis=1) - groups
    cnt = groups[:, experts].T
    start = starts[:, experts].T
    off = jnp.cumsum(cnt, axis=1) - cnt
    total = jnp.sum(cnt, axis=1)
    g = jnp.arange(max_groups, dtype=I32)
    pos = jnp.full((experts.shape[0], max_groups), length - GRP, I32)
    for s in range(n_src):
        rel = g[None] - off[:, s:s + 1]
        inside = (rel >= 0) & (rel < cnt[:, s:s + 1])
        pos = jnp.where(inside, s * length + (start[:, s:s + 1] + rel) * GRP, pos)
    per_tile = ROWS // GRP
    tiles = jnp.maximum(1, (total + per_tile - 1) // per_tile)
    ends = jnp.cumsum(tiles)
    n_tiles = ends[-1]
    most = experts.shape[0] * (max_groups // per_tile) + 2
    t = jnp.minimum(jnp.arange(most, dtype=I32), n_tiles - 1)
    slot = jnp.sum((t[:, None] >= ends[None]).astype(I32), axis=1)
    first = jnp.sum(jnp.where(jnp.arange(experts.shape[0])[None] == slot[:, None], (ends - tiles)[None], 0), axis=1)
    goff = slot * max_groups + (t - first) * per_tile
    bounds = jnp.concatenate([jnp.zeros((1,), I32), ends])
    return bounds, goff, pos.reshape(-1), idx.reshape(-1), gts.reshape(-1)


def expert_kernel(cfg, *refs):
    fwd, bwd, own, n_tok, d, ff = cfg
    refs = list(refs)
    take = lambda n: [refs.pop(0) for _ in range(n)]
    bound_ref, goff_ref, gbase_ref, idx_ref, gate_ref, _ = take(6)
    u_ref = take(1)[0]
    dy_ref = take(1)[0] if bwd else None
    wg_ref, wu_ref, wd_ref = take(3)
    prev = take(3) if bwd and not own else None
    y_out = take(1)[0] if fwd else None
    du_out = take(1)[0] if bwd and own else None
    grads = take(3) if bwd else None
    tab_u = take(1)[0]
    tab_dy = take(1)[0] if bwd else None
    acc_y = take(1)[0] if fwd else None
    acc_du = take(1)[0] if bwd and own else None
    gat_u = take(1)[0]
    gat_c = take(1)[0] if bwd else None
    row_o = take(1)[0] if fwd else None
    row_v = take(1)[0] if bwd and own else None
    x_u = take(1)[0]
    x_c = take(1)[0] if bwd else None
    a_ref, b_ref = take(2)
    dh_ref = take(1)[0] if bwd else None
    h_ref = take(1)[0]
    da_ref, db_ref = take(2) if bwd else (None, None)
    sums = take(3) if bwd and not own else grads
    stage, sem = take(2) if own else (None, None)

    step = pl.program_id(0)
    n_grp = ROWS // GRP
    n_col = cdiv(d, LANES)
    widths = [min(LANES, d - LANES * j) for j in range(n_col)]
    outs = [(acc, row) for acc, row in ((acc_y, row_o), (acc_du, row_v)) if acc is not None]

    def aligned(v):
        return pl.multiple_of(v, 4)

    def gather(tile, q):
        pos = gbase_ref[goff_ref[tile] + q]
        for k in range(GRP):
            i = aligned(idx_ref[pos + k])
            dst = pl.ds(aligned((q * GRP + k) * 4), 4)
            gat_u[dst, :] = tab_u[pl.ds(i, 4), :]
            if bwd:
                gat_c[dst, :] = tab_dy[pl.ds(i, 4), :] * gate_ref[pos + k]

    def scatter(tile, q):
        pos = gbase_ref[goff_ref[tile] + q]
        new = []
        where = [pl.ds(aligned(idx_ref[pos + k]), 4) for k in range(GRP)]
        for k in range(GRP):
            gate = gate_ref[pos + k]
            src = pl.ds(aligned((q * GRP + k) * 4), 4)
            new.append([acc[where[k], :] + gate * row[src, :] for acc, row in outs])
        for k in range(GRP):
            for (acc, _), value in zip(outs, new[k]):
                acc[where[k], :] = value

    def convert():
        for gat, x in ((gat_u, x_u), (gat_c, x_c)):
            if gat is None:
                continue
            for j, w in enumerate(widths):
                for r in range(0, ROWS, 64):
                    rows = gat[pl.ds(4 * r + j, 64, stride=4), :]
                    x[r:r + 64, LANES * j:LANES * j + w] = rows[:, :w].astype(BF16)

    @pl.when(step == 0)
    def _():
        def fill(c, _):
            r = pl.multiple_of(c * 64, 64)
            for src, tab in ((u_ref, tab_u), (dy_ref, tab_dy)):
                if src is None:
                    continue
                for j, w in enumerate(widths):
                    vals = src[pl.ds(r, 64), LANES * j:LANES * j + w].astype(F32)
                    tab[pl.ds(4 * r + j, 64, stride=4), 0:w] = vals
            return 0

        lax.fori_loop(0, n_tok // 64, fill, 0)
        for tab in (tab_u, tab_dy):
            if tab is not None:
                tab[4 * n_tok:, :] = jnp.zeros((tab.shape[0] - 4 * n_tok, LANES), F32)
        for acc, row in outs:
            def clear(c, _, acc=acc):
                acc[pl.ds(pl.multiple_of(c * 512, 512), 512), :] = jnp.zeros((512, LANES), F32)
                return 0

            lax.fori_loop(0, 4 * n_tok // 512, clear, 0)
            acc[4 * n_tok:, :] = jnp.zeros((acc.shape[0] - 4 * n_tok, LANES), F32)
            row[...] = jnp.zeros(row.shape, F32)
        lax.fori_loop(0, n_grp, lambda q, _: (gather(0, q), 0)[1], 0)
        convert()

    if bwd:
        if own:
            for g in sums:
                g[...] = jnp.zeros(g.shape, F32)
        else:
            for g, p in zip(sums, prev):
                g[...] = p[...]

    dot = functools.partial(lax.dot_general, preferred_element_type=F32)
    nn = (((1,), (0,)), ((), ()))
    nt = (((1,), (1,)), ((), ()))
    tn = (((0,), (0,)), ((), ()))
    def put_rows(row, value):
        value = value.astype(BF16).astype(F32)
        for j, w in enumerate(widths):
            row[pl.ds(j, ROWS, stride=4), 0:w] = value[:, LANES * j:LANES * j + w]

    def tile(t, _):
        for q in range(n_grp):
            if outs:
                scatter(jnp.maximum(t - 1, 0), q)
            gather(t + 1, q)

        a_ref[...] = dot(x_u[...], wg_ref[0, 0], nn)
        b_ref[...] = dot(x_u[...], wu_ref[0, 0], nn)
        if bwd:
            dh_ref[...] = dot(x_c[...], wd_ref[0, 0], nt)
        for r in range(0, ROWS, 32):
            rows = slice(r, r + 32)
            a, b = a_ref[rows, :], b_ref[rows, :]
            sig = 0.5 * jnp.tanh(0.5 * a) + 0.5
            act = a * sig
            h_ref[rows, :] = (act * b).astype(BF16)
            if bwd:
                dh = dh_ref[rows, :]
                slope = sig * (1.0 + a * (1.0 - sig))
                da_ref[rows, :] = (dh * b * slope).astype(BF16)
                db_ref[rows, :] = (dh * act).astype(BF16)

        if fwd:
            put_rows(row_o, dot(h_ref[...], wd_ref[0, 0], nn))
        if bwd:
            if own:
                put_rows(row_v, dot(da_ref[...], wg_ref[0, 0], nt) + dot(db_ref[...], wu_ref[0, 0], nt))
            sums[0][0] += dot(x_u[...], da_ref[...], tn)
            sums[1][0] += dot(x_u[...], db_ref[...], tn)
            sums[2][0] += dot(h_ref[...], x_c[...], tn)
        convert()

        return 0

    lax.fori_loop(bound_ref[step], bound_ref[step + 1], tile, 0)
    if bwd and not own:
        for g, s in zip(grads, sums):
            g[...] = s[...].astype(BF16)

    if outs:
        @pl.when(step == pl.num_programs(0) - 1)
        def _():
            end = bound_ref[step + 1] - 1
            lax.fori_loop(0, n_grp, lambda q, _: (scatter(end, q), 0)[1], 0)
            chunk = stage.shape[1]
            for (acc, _), out in zip(outs, [o for o in (y_out, du_out) if o is not None]):
                copies = [None, None]
                for c in range(n_tok // chunk):
                    s = c % 2
                    if copies[s] is not None:
                        copies[s].wait()
                    for j, w in enumerate(widths):
                        stage[s, :, LANES * j:LANES * j + w] = acc[pl.ds(4 * chunk * c + j, chunk, stride=4), 0:w]
                    copies[s] = pltpu.make_async_copy(stage.at[s], out.at[pl.ds(c * chunk, chunk), :], sem.at[s])
                    copies[s].start()
                for copy in copies:
                    copy.wait()


def run_experts(tables, base, layer, u, dy, weights, prev, fwd, own):
    bounds, goff, gbase, idx, gate = tables
    bwd = dy is not None
    wg, wu, wd = weights
    n_tok, d = u.shape
    ff = wg.shape[3]
    n_exp = wg.shape[1] // 2
    scalars = (bounds, goff, gbase, idx, gate, base)

    whole = pl.BlockSpec((n_tok, d), lambda e, *_: (0, 0), pipeline_mode=pl.Buffered(1))

    def weight_spec(w):
        return pl.BlockSpec((1, 1) + w.shape[2:],
                            lambda e, *scalars: (layer, scalars[-1][0] + e, 0, 0))

    def grad_spec(w):
        return pl.BlockSpec((1,) + w.shape[2:], lambda e, *_: (e, 0, 0))

    operands = [u] + ([dy] if bwd else []) + [wg, wu, wd] + (list(prev) if prev else [])
    in_specs = [whole] + ([whole] if bwd else []) + [weight_spec(w) for w in weights]
    in_specs += [grad_spec(w) for w in weights] if prev else []
    out_shape, out_specs = [], []
    for use in (fwd, bwd and own):
        if use:
            out_shape.append(jax.ShapeDtypeStruct((n_tok, d), F32))
            out_specs.append(pl.BlockSpec(memory_space=pl.ANY))
    if bwd:
        for w in weights:
            out_shape.append(jax.ShapeDtypeStruct((n_exp,) + w.shape[2:], F32 if own else BF16))
            out_specs.append(grad_spec(w))
    table = pltpu.VMEM((4 * n_tok + 32, LANES), F32)
    rows = pltpu.VMEM((4 * ROWS, LANES), F32)
    mid = lambda dt: pltpu.VMEM((ROWS, ff), dt)
    x = pltpu.VMEM((ROWS, d), BF16)
    two = 1 + bwd
    scratch = [table] * two + [table] * (fwd + (bwd and own)) + [rows] * two + [rows] * (fwd + (bwd and own))
    scratch += [x] * two + [mid(F32)] * (2 + bwd) + [mid(BF16)] * (1 + 2 * bwd)
    if bwd and not own:
        scratch += [pltpu.VMEM((1,) + w.shape[2:], F32) for w in weights]
    if own:
        scratch += [pltpu.VMEM((2, 256, d), F32), pltpu.SemaphoreType.DMA((2,))]
    passes = (3 * fwd + (0 if fwd else 2)) + bwd * (4 + 2 * own)
    flops = 2 * d * ff * passes * n_tok * 2
    return pl.pallas_call(
        functools.partial(expert_kernel, (fwd, bwd, own, n_tok, d, ff)),
        out_shape=out_shape,
        grid_spec=pltpu.PrefetchScalarGridSpec(
            num_scalar_prefetch=6, grid=(n_exp,), in_specs=in_specs, out_specs=out_specs,
            scratch_shapes=scratch),
        compiler_params=pltpu.CompilerParams(dimension_semantics=("arbitrary",), vmem_limit_bytes=VMEM_LIMIT),
        cost_estimate=pl.CostEstimate(flops=flops, bytes_accessed=3 * 2 * n_exp * d * ff, transcendentals=0),
        name=f"experts_{'f' if fwd else ''}{'b' if bwd else ''}_{'own' if own else 'other'}_{layer}",
    )(*scalars, *operands)


def solution(mesh):
    ep_size, dp_size = mesh.shape['ep'], mesh.shape['dp']
    sub = Mesh(mesh.devices.reshape(ep_size, dp_size // 2, 2), ('ep', 'x', 'core'))
    tok_axes = ('x', 'core', 'ep')
    tok_spec = P(tok_axes, None)
    route_spec = P(None, tok_axes, None)
    whole_spec = P(None, None, None)
    expert_spec = P(None, 'ep', None, None)
    half_axes = ('core', 'ep')

    def device_step(tokens, d_out, expert_ids, gate_vals, w_mix, w_gate, w_up, w_down):
        n_layers = w_mix.shape[0]
        n_tok, d = tokens.shape
        top = expert_ids.shape[2]
        n_exp = w_gate.shape[1] * ep_size
        n_mine = w_gate.shape[1] // 2
        n_src = 2 * ep_size
        cap = CAP_FACTOR * n_tok * top // n_exp
        max_groups = cdiv(n_src * cdiv(cap, GRP), ROWS // GRP) * (ROWS // GRP)
        ix, ic, ie = lax.axis_index('x'), lax.axis_index('core'), lax.axis_index('ep')
        base = (ic * n_mine)[None].astype(I32)
        experts = ie * w_gate.shape[1] + ic * n_mine + jnp.arange(n_mine, dtype=I32)
        weights = (w_gate, w_up, w_down)

        tok, gts, groups = local_lists(expert_ids, gate_vals, n_exp)
        length = tok.shape[1]
        packed = jnp.concatenate([tok.astype(F32), gts, groups.astype(F32)], axis=1)
        packed = lax.all_gather(packed, tok_axes, axis=0, tiled=False)
        packed = packed.reshape(2, n_src, n_layers, -1)

        def tables(layer, other):
            part = lax.dynamic_index_in_dim(packed, (1 - ix) if other else ix, 0, keepdims=False)[:, layer]
            tk = part[:, :length].astype(I32)
            gr = part[:, 2 * length:].astype(I32)
            return half_tables(tk, part[:, length:2 * length], gr, experts, n_tok, max_groups)

        def own_half(block):
            return lax.all_gather(block, half_axes, axis=0, tiled=True)

        def other_half(own):
            mine = lax.dynamic_slice_in_dim(own, ic * 2 * n_tok, 2 * n_tok, 0)
            got = lax.ppermute(mine, 'x', [(0, 1), (1, 0)])
            return lax.all_gather(got, 'core', axis=0, tiled=True)

        def mix(x, w):
            return (x.astype(F32) + jnp.dot(x, w, preferred_element_type=F32)).astype(BF16)

        def mix_back(du, w):
            return (du.astype(F32) + jnp.einsum('te,de->td', du, w, preferred_element_type=F32)).astype(BF16)

        def my_block(half):
            return lax.dynamic_slice_in_dim(half, (ic * ep_size + ie) * n_tok, n_tok, 0)

        def reduce_half(part):
            return lax.psum_scatter(part, half_axes, scatter_dimension=0, tiled=True)

        tabs = [[tables(layer, other) for other in (False, True)] for layer in range(n_layers)]

        x0 = own_half(tokens)
        u0 = mix(x0, w_mix[0])
        (part,) = run_experts(tabs[0][0], base, 0, u0, None, weights, None, True, True)
        y0 = (my_block(u0).astype(F32) + reduce_half(part)).astype(BF16)
        x1 = own_half(y0)
        u1 = mix(x1, w_mix[1])
        dy = own_half(d_out)
        part, dpart, *g1 = run_experts(tabs[1][0], base, 1, u1, dy, weights, None, True, True)
        u1o = mix(other_half(x1), w_mix[1])
        dyo = other_half(dy)
        g1 = run_experts(tabs[1][1], base, 1, u1o, dyo, weights, g1, False, False)
        y1 = (my_block(u1).astype(F32) + reduce_half(part)).astype(BF16)
        du1 = (d_out.astype(F32) + reduce_half(dpart)).astype(BF16)
        dx1 = mix_back(du1, w_mix[1])
        dy = own_half(dx1)
        dpart, *g0 = run_experts(tabs[0][0], base, 0, u0, dy, weights, None, False, True)
        u0o = mix(other_half(x0), w_mix[0])
        dyo = other_half(dy)
        g0 = run_experts(tabs[0][1], base, 0, u0o, dyo, weights, g0, False, False)
        du0 = (dx1.astype(F32) + reduce_half(dpart)).astype(BF16)
        dx0 = mix_back(du0, w_mix[0])

        g_mix = jnp.stack([jnp.einsum('td,te->de', x, du, preferred_element_type=F32)
                           for x, du in ((tokens, du0), (y0, du1))])
        g_mix = lax.psum(g_mix, ('x', 'core', 'ep')).astype(BF16)
        outs = [lax.all_gather(jnp.stack([a, b]), 'core', axis=1, tiled=True) for a, b in zip(g0, g1)]
        return (y1, dx0, g_mix, *outs)

    return jax.shard_map(device_step, mesh=sub,
                         in_specs=(tok_spec, tok_spec, route_spec, route_spec, whole_spec,
                                   expert_spec, expert_spec, expert_spec),
                         out_specs=(tok_spec, tok_spec, whole_spec, expert_spec, expert_spec, expert_spec),
                         check_vma=False)
```

time: 4780 us -> 1170 us (0.24)
  waiting for transfers between devices: 1790 us -> 389 us
  local copies, waits for them, and re-layouts: 1520 us -> 240 us
  matrix products: 504 us -> 45 us
  blocking collectives: 488 us -> 75.3 us
  Pallas kernels: 0 us -> 343 us
  other arithmetic: 368 us -> 48.7 us
  starting transfers between devices: 68.5 us -> 7.09 us
    gather x26 -> x8, local copies, waits for them, and re-layouts: 1090 us -> 4.49 us  [the longest x4 2.25 us: half_tables(): cnt = groups[:, experts].T]
    psum x2 -> x0, waiting for transfers between devices: 1040 us -> none  [the longest x1 1020 us: layer_backward(): g_gate = lax.psum(g_gate, 'dp')]
    all_to_all x6 -> x0, waiting for transfers between devices: 753 us -> none  [the longest x1 215 us: layer_backward(): recv_grad = lax.all_to_all(send_grad, 'ep', 0, 0, tiled=True)]
    all_to_all x2 -> x0, blocking collectives: 488 us -> none  [the longest x1 247 us: layer_forward(): recv_buf = lax.all_to_all(send_buf, 'ep', 0, 0, tiled=True)]
    dot_general x24 -> x8, matrix products: 504 us -> 45 us  [the longest x4 31.5 us: mix(): jnp.dot(x, w, preferred_element_type=F32)]
    pallas_call x0 -> x5, Pallas kernels: none -> 343 us  [run_experts(): pl.pallas_call(functools.partial(expert_kernel, (fwd, bwd, own, n_tok, d,...]
    reduce_scatter x0 -> x4, waiting for transfers between devices: none -> 184 us  [reduce_half(): return lax.psum_scatter(part, half_axes, scatter_dimension=0, tiled=True)]
    ppermute x0 -> x4, waiting for transfers between devices: none -> 156 us  [other_half(): got = lax.ppermute(mine, 'x', [(0, 1), (1, 0)])]
  transfers between devices with their start and end apart: 8 -> 20, of which waited for: 7 -> 8; matrix products, arithmetic and copies ran while one was open for 19% -> 22% of each run, Pallas kernels for 0% -> 17%
where the time goes in v1:
time: 1170 us
  waiting for transfers between devices  389 us (33%)
  Pallas kernels  343 us (29%)
  local copies, waits for them, and re-layouts  240 us (21%)
  blocking collectives  75.3 us (6%)
  other arithmetic  48.7 us (4%)
  matrix products  45 us (4%)
  between operations  17.5 us (1%)
    pallas_call x5, Pallas kernels, run_experts(): pl.pallas_call(functools.partial(expert_kernel, (fwd, bwd, own, n_tok, d,...  343 us
    reduce_scatter x4, waiting for transfers between devices, reduce_half(): return lax.psum_scatter(part, half_axes, scatter_dimension=0, tiled=True)  184 us
    ppermute x4, waiting for transfers between devices, other_half(): got = lax.ppermute(mine, 'x', [(0, 1), (1, 0)])  156 us
    unnamed x29, local copies, waits for them, and re-layouts  140 us
    psum x1, blocking collectives, device_step(): g_mix = lax.psum(g_mix, ('x', 'core', 'ep')).astype(BF16)  75.3 us
    all_gather x4, waiting for transfers between devices, own_half(): return lax.all_gather(block, half_axes, axis=0, tiled=True)  48.7 us
    sort x2, local copies, waits for them, and re-layouts, local_lists(): keys, gts = lax.sort((keys, gts), dimension=1, num_keys=1)  33.8 us
    dot_general x4, matrix products, mix(): jnp.dot(x, w, preferred_element_type=F32)  31.5 us
  transfers between devices with their start and end apart: 20, of which 8 were waited for; matrix products, arithmetic and copies ran while one was open for 22% of the time, Pallas kernels for 17%

profile of v1, /device:TPU:0, one launch (start us, length us, event | category | flops | bytes accessed | tf_op | source)
XLA Modules:
  0.0 1165.7 jit_solution(8366041222000996032)
XLA Ops:
  13.7 33.7 %sort.17.cloned.1.call-done = (s32[2,8704]{1,0:T(2,128)}, f32[2,8704]{1,0:T(2,128)}) async-done(((s32[2,8704]{1,0:T(2,128)}, f32[2,8704]{1,0:T(2,128)}), (s32[2,8704]{1,0:T(2,128)}, f32[2,8704]{1,0:T(2,128)})) %sort.17.cloned.1.call-update) | async-done | bytes 139280 | tf_op jit(solution)/shard_map/sort | solution.py:38
  51.7 28.0 %copy.149.refs_7_.refs_8_ = bf16[2,32,448,320]{3,2,1,0:T(8,128)(2,1)} copy(bf16[2,32,448,320]{2,3,1,0:T(8,128)(2,1)} %param.13) | data formatting | bytes 36700160 | tf_op args[5]
  79.7 28.0 %copy.150.refs_8_.refs_9_ = bf16[2,32,448,320]{3,2,1,0:T(8,128)(2,1)} copy(bf16[2,32,448,320]{2,3,1,0:T(8,128)(2,1)} %param.14) | data formatting | bytes 36700160 | tf_op args[6]
  118.1 8.0 add_convert_fusion.3.refs_6_
  126.0 45.0 %experts_f_own_0.1 = f32[4096,448]{1,0:T(8,128)} custom-call(s32[17]{0:T(128)} %pad_add_fusion.3.refs_0_, s32[66]{0:T(128)} %multiply_add_fusion.3.refs_1_, s32[3072]{0:T(1024)} %reshape.654.refs_2_, s32[34816]{0:T(1024)} %reshape.635.refs_3_, f32[34816]{0:T(1024)} %reshape.636.refs_4_, s32[1]{0:T(128)} %bitcast.9.refs_5_, ...), custom_call_target="tpu_custom_call" | custom-call | flops 7046430720 | bytes 13762560 | tf_op jit(solution)/shard_map/experts_f_own_0/pallas_call | solution.py:286
  171.1 75.8 %reduce-scatter.5.cloned.1.call-done = f32[1024,448]{1,0:T(8,128)} async-done(((f32[4096,448]{1,0:T(8,128)}), f32[1024,448]{1,0:T(8,128)}) %reduce-scatter.5.cloned.1.call-update) | async-done | bytes 1835024 | tf_op jit(solution)/shard_map/reduce_scatter | solution.py:352
  258.2 23.6 %all-gather.17.cloned.1.call-done = bf16[4096,448]{1,0:T(8,128)(2,1)} async-done(((bf16[1024,448]{1,0:T(8,128)(2,1)}), bf16[4096,448]{1,0:T(8,128)(2,1)}) %all-gather.17.cloned.1.call-update) | async-done | bytes 3670032 | tf_op jit(solution)/shard_map/all_gather | solution.py:335
  289.7 25.0 %all-gather.19.cloned.1.call-done.refs_7_ = bf16[4096,448]{1,0:T(8,128)(2,1)} async-done(((bf16[1024,448]{1,0:T(8,128)(2,1)}), bf16[4096,448]{1,0:T(8,128)(2,1)}) %all-gather.19.cloned.1.call-update) | async-done | bytes 3670032 | tf_op jit(solution)/shard_map/all_gather | solution.py:335
  314.7 101.0 %experts_fb_own_1.1 = (f32[4096,448]{1,0:T(8,128)}, f32[4096,448]{1,0:T(8,128)}, f32[16,448,320]{2,1,0:T(8,128)}, f32[16,448,320]{2,1,0:T(8,128)}, f32[16,320,448]{2,1,0:T(8,128)}) custom-call(s32[17]{0:T(128)} %pad_add_fusion.2.refs_0_, s32[66]{0:T(128)} %multiply_add_fusion.2.refs_1_, s32[3072]{0:T(1024)} %reshape.655.refs_2_, s32[34816]{0:T(1024)} %reshape.638.refs_3_, ...), custom_call_target="tpu_custom_call" | custom-call | flops 21139292160 | bytes 13762560 | tf_op jit(solution)/shard_map/experts_fb_own_1/pallas_call | solution.py:286
  415.8 108.0 %reduce-scatter.9.cloned.1.call-done = f32[1024,448]{1,0:T(8,128)} async-done(((f32[4096,448]{1,0:T(8,128)}), f32[1024,448]{1,0:T(8,128)}) %reduce-scatter.9.cloned.1.call-update) | async-done | bytes 1835024 | tf_op jit(solution)/shard_map/reduce_scatter | solution.py:352
  536.3 40.0 %collective-permute-done = bf16[2048,448]{0,1:T(8,128)(2,1)} collective-permute-done((bf16[2048,448]{0,1:T(8,128)(2,1)}, bf16[2048,448]{0,1:T(8,128)(2,1)}, u32[]{:S(2)}, u32[]{:S(2)}) %collective-permute-start) | collective-permute-done | bytes 1835040 | tf_op jit(solution)/shard_map/ppermute | solution.py:339
  588.7 39.3 %collective-permute-done.2 = bf16[2048,448]{0,1:T(8,128)(2,1)} collective-permute-done((bf16[2048,448]{0,1:T(8,128)(2,1)}, bf16[2048,448]{0,1:T(8,128)(2,1)}, u32[]{:S(2)}, u32[]{:S(2)}) %collective-permute-start.2) | collective-permute-done | bytes 1835040 | tf_op jit(solution)/shard_map/ppermute | solution.py:339
  640.2 38.6 %collective-permute-done.3 = bf16[2048,448]{0,1:T(8,128)(2,1)} collective-permute-done((bf16[2048,448]{0,1:T(8,128)(2,1)}, bf16[2048,448]{0,1:T(8,128)(2,1)}, u32[]{:S(2)}, u32[]{:S(2)}) %collective-permute-start.3) | collective-permute-done | bytes 1835040 | tf_op jit(solution)/shard_map/ppermute | solution.py:339
  691.1 37.9 %collective-permute-done.1 = bf16[2048,448]{0,1:T(8,128)(2,1)} collective-permute-done((bf16[2048,448]{0,1:T(8,128)(2,1)}, bf16[2048,448]{0,1:T(8,128)(2,1)}, u32[]{:S(2)}, u32[]{:S(2)}) %collective-permute-start.1) | collective-permute-done | bytes 1835040 | tf_op jit(solution)/shard_map/ppermute | solution.py:339
  733.8 76.8 %experts_b_own_0.1 = (f32[4096,448]{1,0:T(8,128)}, f32[16,448,320]{2,1,0:T(8,128)}, f32[16,448,320]{2,1,0:T(8,128)}, f32[16,320,448]{2,1,0:T(8,128)}) custom-call(s32[17]{0:T(128)} %pad_add_fusion.3.refs_0_, s32[66]{0:T(128)} %multiply_add_fusion.3.refs_1_, s32[3072]{0:T(1024)} %reshape.654.refs_2_, s32[34816]{0:T(1024)} %reshape.635.refs_3_, ...), custom_call_target="tpu_custom_call" | custom-call | flops 18790481920 | bytes 13762560 | tf_op jit(solution)/shard_map/experts_b_own_0/pallas_call | solution.py:286
  841.3 60.3 %experts_b_other_1.1 = (bf16[16,448,320]{2,1,0:T(8,128)(2,1)}, bf16[16,448,320]{2,1,0:T(8,128)(2,1)}, bf16[16,320,448]{2,1,0:T(8,128)(2,1)}) custom-call(s32[17]{0:T(128)} %pad_add_fusion.refs_0_, s32[66]{0:T(128)} %multiply_add_fusion.refs_1_, s32[3072]{0:T(1024)} %reshape.657.refs_2_, s32[34816]{0:T(1024)} %reshape.644.refs_3_, f32[34816]{0:T(1024)} %reshape.645.refs_4_, ...), custom_call_target="tpu_custom_call" | custom-call | flops 14092861440 | bytes 13762560 | tf_op jit(solution)/shard_map/experts_b_other_1/pallas_call | solution.py:286
  901.6 60.3 %experts_b_other_0.1 = (bf16[16,448,320]{2,1,0:T(8,128)(2,1)}, bf16[16,448,320]{2,1,0:T(8,128)(2,1)}, bf16[16,320,448]{2,1,0:T(8,128)(2,1)}) custom-call(s32[17]{0:T(128)} %pad_add_fusion.1.refs_0_, s32[66]{0:T(128)} %multiply_add_fusion.1.refs_1_, s32[3072]{0:T(1024)} %reshape.656.refs_2_, s32[34816]{0:T(1024)} %reshape.641.refs_3_, ...), custom_call_target="tpu_custom_call" | custom-call | flops 14092861440 | bytes 13762560 | tf_op jit(solution)/shard_map/experts_b_other_0/pallas_call | solution.py:286
  961.8 10.2 pad_maximum_fusion.1
  972.1 10.2 pad_maximum_fusion
  982.6 9.1 pad_maximum_fusion.2
  1009.1 75.3 %all-reduce.2 = bf16[2,448,448]{1,2,0:T(8,128)(2,1)S(1)} all-reduce(f32[2,448,448]{1,2,0:T(8,128)S(1)} %pad_maximum_fusion.3), channel_id=1, replica_groups=mesh['ep'=2,'x'=2,'core'=2] {'x','core','ep'}, use_global_device_ids=true, to_apply=%region_18.19 | all-reduce | flops 401408 | bytes 2408448 | tf_op jit(solution)/shard_map/psum | solution.py:380
  1085.7 27.8 %copy.189 = bf16[2,32,448,320]{2,3,1,0:T(8,128)(2,1)} copy(bf16[2,32,448,320]{3,2,1,0:T(8,128)(2,1)} %all-gather.33.cloned.1.call-done) | data formatting | bytes 36700160
  1113.5 27.8 %copy.188 = bf16[2,32,448,320]{2,3,1,0:T(8,128)(2,1)} copy(bf16[2,32,448,320]{3,2,1,0:T(8,128)(2,1)} %all-gather.31.cloned.1.call-done) | data formatting | bytes 36700160
  1141.3 17.5 %copy.204 = bf16[2,32,320,448]{3,2,1,0:T(8,128)(2,1)} copy(bf16[2,32,320,448]{3,2,1,0:T(8,128)(2,1)} %all-gather.35.cloned.1.call-done) | data formatting | bytes 36700160
  (227 shorter events, 141.2 us)
Async XLA Ops:
  7.2 43.1 %copy-start.3 = (bf16[1024,448]{0,1:T(8,128)(2,1)S(1)}, bf16[1024,448]{0,1:T(8,128)(2,1)}, u32[]{:S(2)}) copy-start(bf16[1024,448]{0,1:T(8,128)(2,1)} %param.8) | copy-start | bytes 2752516
  13.6 94.1 %all-gather.37.cloned.1.call-start = ((), (), s32[]{:S(2)}) async-start(), calls=%async_computation.19 | async-start | bytes 1262592 | tf_op jit(solution)/shard_map/all_gather | solution.py:325
  50.2 67.9 %all-gather.15.cloned.1.call-start = ((), (), s32[]{:S(2)}) async-start(), calls=%async_computation.4 | async-start | bytes 5242880 | tf_op jit(solution)/shard_map/all_gather | solution.py:335
  51.6 195.3 %reduce-scatter.5.cloned.1.call-start = ((), (), s32[]{:S(2)}) async-start(), calls=%async_computation.5 | async-start | bytes 10485760 | tf_op jit(solution)/shard_map/reduce_scatter | solution.py:352
  171.0 79.2 %copy-start.5 = (bf16[1024,448]{0,1:T(8,128)(2,1)S(1)}, bf16[1024,448]{0,1:T(8,128)(2,1)}, u32[]{:S(2)}) copy-start(bf16[1024,448]{0,1:T(8,128)(2,1)} %param.9) | copy-start | bytes 2752516
  171.0 110.8 %all-gather.17.cloned.1.call-start = ((), (), s32[]{:S(2)}) async-start(), calls=%async_computation.6 | async-start | bytes 5242880 | tf_op jit(solution)/shard_map/all_gather | solution.py:335
  250.1 64.6 %all-gather.19.cloned.1.call-start = ((), (), s32[]{:S(2)}) async-start(), calls=%async_computation.7 | async-start | bytes 5242880 | tf_op jit(solution)/shard_map/all_gather | solution.py:335
  251.5 272.3 %reduce-scatter.9.cloned.1.call-start = ((), (), s32[]{:S(2)}) async-start(), calls=%async_computation.9 | async-start | bytes 10485760 | tf_op jit(solution)/shard_map/reduce_scatter | solution.py:352
  415.7 108.1 %copy-start.1 = (bf16[1024,448]{1,0:T(8,128)(2,1)S(1)}, bf16[1024,448]{1,0:T(8,128)(2,1)}, u32[]{:S(2)}) copy-start(bf16[1024,448]{1,0:T(8,128)(2,1)} %copy.155) | copy-start | bytes 2752516
  415.7 108.1 %copy-start.6 = (bf16[2,448,448]{2,1,0:T(8,128)(2,1)S(1)}, bf16[2,448,448]{2,1,0:T(8,128)(2,1)}, u32[]{:S(2)}) copy-start(bf16[2,448,448]{2,1,0:T(8,128)(2,1)} %param.12) | copy-start | bytes 2408452
  415.7 267.0 %all-gather.21.cloned.1.call-start = ((), (), s32[]{:S(2)}) async-start(), calls=%async_computation.10 | async-start | bytes 5242880 | tf_op jit(solution)/shard_map/all_gather | solution.py:335
  527.8 297.8 %all-gather.23.cloned.1.call-start = ((), (), s32[]{:S(2)}) async-start(), calls=%async_computation.12 | async-start | bytes 6291456 | tf_op jit(solution)/shard_map/all_gather | solution.py:340
  534.8 41.5 %collective-permute-start = (bf16[2048,448]{0,1:T(8,128)(2,1)}, bf16[2048,448]{0,1:T(8,128)(2,1)}, u32[]{:S(2)}, u32[]{:S(2)}) collective-permute-start(bf16[2048,448]{0,1:T(8,128)(2,1)} %copy.168), channel_id=1, source_target_pairs={{0,2},{2,0},{1,3},{3,1},{4,6},{6,4},{5,7},{7,5}} | collective-permute-start | bytes 5505032 | tf_op jit(solution)/shard_map/ppermute | solution.py:339
  580.2 253.3 %all-gather.27.cloned.1.call-start = ((), (), s32[]{:S(2)}) async-start(), calls=%async_computation.14 | async-start | bytes 6291456 | tf_op jit(solution)/shard_map/all_gather | solution.py:340
  587.2 40.8 %collective-permute-start.2 = (bf16[2048,448]{0,1:T(8,128)(2,1)}, bf16[2048,448]{0,1:T(8,128)(2,1)}, u32[]{:S(2)}, u32[]{:S(2)}) collective-permute-start(bf16[2048,448]{0,1:T(8,128)(2,1)} %copy.178), channel_id=1, source_target_pairs={{0,2},{2,0},{1,3},{3,1},{4,6},{6,4},{5,7},{7,5}} | collective-permute-start | bytes 5505032 | tf_op jit(solution)/shard_map/ppermute | solution.py:339
  631.8 209.5 %all-gather.29.cloned.1.call-start = ((), (), s32[]{:S(2)}) async-start(), calls=%async_computation.15 | async-start | bytes 6291456 | tf_op jit(solution)/shard_map/all_gather | solution.py:340
  638.8 40.0 %collective-permute-start.3 = (bf16[2048,448]{0,1:T(8,128)(2,1)}, bf16[2048,448]{0,1:T(8,128)(2,1)}, u32[]{:S(2)}, u32[]{:S(2)}) collective-permute-start(bf16[2048,448]{0,1:T(8,128)(2,1)} %copy.181), channel_id=1, source_target_pairs={{0,2},{2,0},{1,3},{3,1},{4,6},{6,4},{5,7},{7,5}} | collective-permute-start | bytes 5505032 | tf_op jit(solution)/shard_map/ppermute | solution.py:339
  682.7 218.9 %all-gather.25.cloned.1.call-start = ((), (), s32[]{:S(2)}) async-start(), calls=%async_computation.13 | async-start | bytes 6291456 | tf_op jit(solution)/shard_map/all_gather | solution.py:340
  689.7 39.3 %collective-permute-start.1 = (bf16[2048,448]{0,1:T(8,128)(2,1)}, bf16[2048,448]{0,1:T(8,128)(2,1)}, u32[]{:S(2)}, u32[]{:S(2)}) collective-permute-start(bf16[2048,448]{0,1:T(8,128)(2,1)} %copy.171), channel_id=1, source_target_pairs={{0,2},{2,0},{1,3},{3,1},{4,6},{6,4},{5,7},{7,5}} | collective-permute-start | bytes 5505032 | tf_op jit(solution)/shard_map/ppermute | solution.py:339
  732.8 258.9 %reduce-scatter.7.cloned.1.call-start = ((), (), s32[]{:S(2)}) async-start(), calls=%async_computation.8 | async-start | bytes 10485760 | tf_op jit(solution)/shard_map/reduce_scatter | solution.py:352
  733.6 265.9 %reduce-scatter.11.cloned.1.call-start = ((), (), s32[]{:S(2)}) async-start(), calls=%async_computation.11 | async-start | bytes 10485760 | tf_op jit(solution)/shard_map/reduce_scatter | solution.py:352
  810.7 275.0 %all-gather.33.cloned.1.call-start = ((), (), s32[]{:S(2)}) async-start(), calls=%async_computation.17 | async-start | bytes 33030144 | tf_op jit(solution)/shard_map/all_gather | solution.py:381
  972.0 141.5 %all-gather.31.cloned.1.call-start = ((), (), s32[]{:S(2)}) async-start(), calls=%async_computation.16 | async-start | bytes 33030144 | tf_op jit(solution)/shard_map/all_gather | solution.py:381
  982.3 159.0 %all-gather.35.cloned.1.call-start = ((), (), s32[]{:S(2)}) async-start(), calls=%async_computation.18 | async-start | bytes 31457280 | tf_op jit(solution)/shard_map/all_gather | solution.py:381
  (5 other events, 74.8 us)
Sparse Core Ops, SparseCore 0:
  13.8 33.5 sort.19.cloned.1.call-done
  50.3 20.6 all-gather.36
  73.1 31.4 all-gather.14
  171.1 75.7 reduce-scatter.4
  250.2 31.5 all-gather.16
  283.2 31.5 all-gather.18
  415.9 107.8 reduce-scatter.8
  528.0 31.4 all-gather.20
  580.3 11.2 all-gather.22
  631.9 11.2 all-gather.26
  682.8 11.2 all-gather.28
  732.9 11.2 all-gather.24
  746.8 66.2 reduce-scatter.6
  815.5 73.2 reduce-scatter.10
  972.1 73.5 all-gather.32
  1047.7 38.4 all-gather.30
  1087.5 36.5 all-gather.34
  (1 shorter events, 0.0 us)

commit v2 on v0

v2 whole, which is shorter than its diff:
```python
import functools

import jax
import jax.numpy as jnp
from jax import lax
from jax.experimental import pallas as pl
from jax.experimental.pallas import tpu as pltpu
from jax.sharding import Mesh, PartitionSpec as P

F32, BF16, I32 = jnp.float32, jnp.bfloat16, jnp.int32
MESH = pl.DeviceIdType.MESH
ROWS = 384
GRP = 8
PITCH = 8
HALF = 4
CAP_FACTOR = 3
LANES = 128
N_SRC = 4
VMEM_LIMIT = 62 * 1024 * 1024


def cdiv(a, b):
    return (a + b - 1) // b


def spans(d):
    return [(LANES * j, min(LANES, d - LANES * j)) for j in range(cdiv(d, LANES))]


def sorted_list(expert_ids, gate_vals):
    n_tok, top = expert_ids.shape
    n = n_tok * top
    keys = expert_ids.reshape(n) * n + jnp.arange(n, dtype=I32)
    keys, gates = lax.sort((keys, gate_vals.reshape(n)), num_keys=1)
    return ((keys % n) // top).astype(F32), gates


def scalar_tables(cnt, first, n_local, core, list_len, max_groups):
    n_rel, n_layers, _ = cnt.shape
    n_mine = n_local // 2
    starts = jnp.cumsum(cnt, axis=2) - cnt
    cnt = lax.dynamic_slice_in_dim(cnt, first, n_local, 2)
    starts = lax.dynamic_slice_in_dim(starts, first, n_local, 2)
    per_tile = ROWS // GRP
    grp = (cnt + GRP - 1) // GRP
    halves = grp.reshape(2, N_SRC, n_layers, n_local).sum(1)
    tiles = jnp.maximum(1, (halves + per_tile - 1) // per_tile)
    load = 3 * tiles[0] + 2 * tiles[1]
    e = jnp.arange(n_local, dtype=I32)
    ahead = (load[:, None, :] > load[:, :, None]) | ((load[:, None, :] == load[:, :, None]) & (e[None, None] < e[None, :, None]))
    rank = jnp.sum(ahead.astype(I32), axis=2)
    k = jnp.arange(n_mine, dtype=I32)
    want = 2 * k + (k + core) % 2
    pick = (rank[:, None, :] == want[None, :, None]).astype(I32)

    def mine(v):
        return jnp.sum(pick * v[..., None, :], axis=-1)

    experts = mine(jnp.broadcast_to(e, (n_layers, n_local)))
    cnt4 = mine(cnt.reshape(2, N_SRC, n_layers, n_local))
    src = jnp.arange(N_SRC, dtype=I32)[None, :, None, None]
    start4 = mine(starts.reshape(2, N_SRC, n_layers, n_local)) + src * list_len
    ng = (cnt4 + GRP - 1) // GRP
    off = jnp.cumsum(ng, axis=1) - ng
    total = jnp.sum(ng, axis=1)
    g = jnp.arange(max_groups, dtype=I32)
    tails = N_SRC * list_len
    pos = jnp.full(total.shape + (max_groups,), tails + n_mine * N_SRC * GRP, I32)
    for s in range(N_SRC):
        rel = g - off[:, s][..., None]
        full = start4[:, s][..., None] + rel * GRP
        tail = tails + (k[None, None, :, None] * N_SRC + s) * GRP
        value = jnp.where(rel * GRP + GRP > cnt4[:, s][..., None], tail, full)
        pos = jnp.where((rel >= 0) & (rel < ng[:, s][..., None]), value, pos)
    n_tiles = jnp.maximum(1, (total + per_tile - 1) // per_tile)
    ends = jnp.cumsum(n_tiles, axis=2)
    most = n_mine * (max_groups // per_tile) + 2
    t = jnp.minimum(jnp.arange(most, dtype=I32), ends[..., -1:] - 1)
    past = (t[..., None] >= ends[:, :, None, :]).astype(I32)
    slot = jnp.sum(past, axis=3)
    before = jnp.max(past * ends[:, :, None, :], axis=3)
    goff = slot * max_groups + (t - before) * per_tile
    bounds = jnp.concatenate([jnp.zeros_like(ends[..., :1]), ends], axis=2)
    parts = [jnp.broadcast_to(experts[None], (2, n_layers, n_mine)), bounds, goff,
             start4.transpose(0, 2, 3, 1).reshape(2, n_layers, -1), cnt4.transpose(0, 2, 3, 1).reshape(2, n_layers, -1),
             pos.reshape(2, n_layers, -1)]
    where, at = [], 0
    for p in parts:
        where.append(at)
        at += p.shape[-1]
    flat = jnp.concatenate(parts, axis=2)
    return flat.reshape(-1), where, at


def expert_kernel(cfg, *refs):
    fwd, bwd, own, mix_dy, n_blk, d, ff, where, at0, list_at, list_len, n_exp, p_f32, n_alias = cfg
    refs = list(refs)
    take = lambda n: [refs.pop(0) for _ in range(n)]
    tab_ref = take(1)[0]
    idx_hbm, gate_hbm = take(2)
    x_refs = take(N_SRC)
    mix_ref = take(1)[0]
    dy_refs = take(N_SRC) if bwd else []
    mixb_ref = take(1)[0] if mix_dy else None
    wg_ref, wu_ref, wd_ref = take(3)
    prev = take(1)[0] if bwd and not own else None
    take(n_alias)
    y_outs = take(N_SRC) if fwd else []
    du_outs = take(N_SRC) if bwd and own else []
    grad = take(1)[0] if bwd and own else None
    finals = take(3) if bwd and not own else None
    sent = take(1)[0] if bwd and not own else None
    table = take(1)[0]
    acc = take(1)[0] if own else None
    gat_u = take(1)[0]
    gat_c = take(1)[0] if bwd else None
    row_o = take(1)[0] if fwd else None
    row_v = take(1)[0] if bwd and own else None
    gu_ref = take(1)[0]
    x_u = take(1)[0]
    x_c = take(1)[0] if bwd else None
    ab_ref = take(1)[0]
    dh_ref = take(1)[0] if bwd else None
    h_ref = take(1)[0]
    dab_ref = take(1)[0] if bwd else None
    sums = take(1)[0] if bwd and not own else None
    idx, gates, list_sem = take(3)
    stage_f, stage_b, out_sem = take(3) if own else (None, None, None)

    step = pl.program_id(0)
    n_grp = ROWS // GRP
    cols = spans(d)
    lo = ff // 256 * 256
    hi = ff - lo
    e_at, b_at, g_at, s_at, c_at, p_at = [at0 + w for w in where]
    outs = [(k, row) for k, row in ((0, row_o), (HALF, row_v)) if row is not None]
    dot = functools.partial(lax.dot_general, preferred_element_type=F32)
    nn = (((1,), (0,)), ((), ()))
    nt = (((1,), (1,)), ((), ()))
    tn = (((0,), (0,)), ((), ()))

    def al(v, m=HALF):
        return pl.multiple_of(v, m)

    def gather(tile, q):
        pos = tab_ref[p_at + tab_ref[g_at + tile] + q]
        for k in range(GRP):
            i = idx[pos + k]
            dst = pl.ds(al((q * GRP + k) * HALF), HALF)
            gat_u[dst, :] = table[pl.ds(al(i), HALF), :]
            if bwd:
                gat_c[dst, :] = table[pl.ds(al(i + HALF), HALF), :] * gates[pos + k]

    def scatter(tile, q):
        pos = tab_ref[p_at + tab_ref[g_at + tile] + q]
        new = []
        at = [idx[pos + k] for k in range(GRP)]
        for k in range(GRP):
            gate = gates[pos + k]
            src = pl.ds(al((q * GRP + k) * HALF), HALF)
            new.append([acc[pl.ds(al(at[k] + o), HALF), :] + gate * row[src, :] for o, row in outs])
        for k in range(GRP):
            for (o, _), value in zip(outs, new[k]):
                acc[pl.ds(al(at[k] + o), HALF), :] = value

    def convert():
        for gat, x in ((gat_u, x_u), (gat_c, x_c)):
            if gat is None:
                continue
            for j, (c, w) in enumerate(cols):
                for r in range(0, ROWS, 64):
                    rows = gat[pl.ds(HALF * r + j, 64, stride=HALF), :]
                    x[r:r + 64, c:c + w] = rows[:, :w].astype(BF16)

    @pl.when(step == 0)
    def _():
        src = pl.ds(list_at, N_SRC * list_len)
        dst = pl.ds(0, N_SRC * list_len)
        copies = [pltpu.make_async_copy(idx_hbm.at[src], idx.at[dst], list_sem.at[0]),
                  pltpu.make_async_copy(gate_hbm.at[src], gates.at[dst], list_sem.at[1])]
        for copy in copies:
            copy.start()
        if own:
            def clear(c, _):
                acc[pl.ds(al(c * 512, 512), 512), :] = jnp.zeros((512, LANES), F32)
                return 0

            lax.fori_loop(0, acc.shape[0] // 512, clear, 0)
            for _, row in outs:
                row[...] = jnp.zeros(row.shape, F32)
        table[PITCH * N_SRC * n_blk:, :] = jnp.zeros((table.shape[0] - PITCH * N_SRC * n_blk, LANES), F32)
        rows = 256
        plan = [(x_refs, mix_ref, nn, 0, fwd)]
        if bwd:
            plan.append((dy_refs, mixb_ref, nt, HALF, own))
        for srcs, m_ref, dims, o, seed in plan:
            for s, ref in enumerate(srcs):
                def fill(c, _, ref=ref, m_ref=m_ref, dims=dims, o=o, seed=seed, s=s):
                    r = al(c * rows, rows)
                    vals = ref[pl.ds(r, rows), :]
                    if m_ref is not None:
                        mixed = vals.astype(F32) + dot(vals, m_ref[...], dims)
                        vals = mixed.astype(BF16)
                    vals = vals.astype(F32)
                    at = PITCH * (s * n_blk + r) + o
                    for j, (cc, w) in enumerate(cols):
                        to = pl.ds(at + j, rows, stride=PITCH)
                        table[to, 0:w] = vals[:, cc:cc + w]
                        if seed and s == 0:
                            acc[to, 0:w] = vals[:, cc:cc + w]
                    return 0

                lax.fori_loop(0, n_blk // rows, fill, 0)
        for copy in copies:
            copy.wait()
        dummy = PITCH * N_SRC * n_blk

        def tail(q, _):
            n = tab_ref[c_at + q]
            left = n % GRP
            p = tab_ref[s_at + q] + n - left
            to = N_SRC * list_len + q * GRP
            for k in range(GRP):
                idx[to + k] = jnp.where(k < left, idx[p + k], dummy)
                gates[to + k] = jnp.where(k < left, gates[p + k], 0.0)
            return 0

        lax.fori_loop(0, n_exp * N_SRC, tail, 0)
        for k in range(GRP):
            idx[N_SRC * (list_len + n_exp * GRP) + k] = dummy
            gates[N_SRC * (list_len + n_exp * GRP) + k] = 0.0
        lax.fori_loop(0, n_grp, lambda q, _: (gather(0, q), 0)[1], 0)
        convert()

    for i, w in enumerate((wg_ref, wu_ref)):
        gu_ref[i * lo:(i + 1) * lo, :] = w[0, 0, 0:lo, :]
        gu_ref[2 * lo + i * hi:2 * lo + (i + 1) * hi, :] = w[0, 0, lo:, :]
    total = grad if own else sums
    if bwd:
        total[...] = jnp.zeros(total.shape, F32) if own else prev[0]

    def put_rows(row, value):
        value = value.astype(BF16).astype(F32)
        for j, (c, w) in enumerate(cols):
            row[pl.ds(j, ROWS, stride=HALF), 0:w] = value[:, c:c + w]

    low = lax.broadcasted_iota(I32, (16, 2 * hi), 1) < hi

    def middle(a, b, dh):
        sig = 0.5 * jnp.tanh(0.5 * a) + 0.5
        act = a * sig
        h = act * b
        if dh is None:
            return h, None, None
        slope = sig * (1.0 + a * (1.0 - sig))
        return h, dh * b * slope, dh * act

    def tile(t, _):
        for q in range(n_grp):
            if outs:
                scatter(jnp.maximum(t - 1, 0), q)
            gather(t + 1, q)
        ab_ref[...] = dot(x_u[...], gu_ref[...], nt)
        if bwd:
            dh_ref[...] = dot(x_c[...], wd_ref[0, 0], nt)
        for r in range(0, ROWS, 16):
            rows = slice(r, r + 16)
            for c in range(0, lo, LANES):
                h, da, db = middle(ab_ref[rows, c:c + LANES], ab_ref[rows, lo + c:lo + c + LANES],
                                   dh_ref[rows, c:c + LANES] if bwd else None)
                h_ref[rows, c:c + LANES] = h.astype(BF16)
                if bwd:
                    dab_ref[rows, c:c + LANES] = da.astype(BF16)
                    dab_ref[rows, lo + c:lo + c + LANES] = db.astype(BF16)
            a = ab_ref[rows, 2 * lo:]
            b = pltpu.roll(a, hi, 1)
            dh = dh_ref[rows, lo:] if bwd else None
            if bwd:
                dh = jnp.concatenate([dh, dh], axis=1)
            h, da, db = middle(a, b, dh)
            h_ref[rows, lo:] = h[:, :hi].astype(BF16)
            if bwd:
                dab_ref[rows, 2 * lo:] = jnp.where(low, da, pltpu.roll(db, hi, 1)).astype(BF16)
        if fwd:
            put_rows(row_o, dot(h_ref[...], wd_ref[0, 0], nn))
        if bwd:
            if own:
                put_rows(row_v, dot(dab_ref[...], gu_ref[...], nn))
            view = total.at[0] if own else total
            view[0:2 * ff, :] += dot(dab_ref[...], x_u[...], tn)
            view[2 * ff:, :] += dot(h_ref[...], x_c[...], tn)
        convert()
        return 0

    lax.fori_loop(tab_ref[b_at + step], tab_ref[b_at + step + 1], tile, 0)
    if bwd and not own:
        for out in ([f.at[0, 0] for f in finals], [sent.at[0, i] for i in range(3)]):
            for i in range(2):
                out[i][0:lo, :] = sums[i * lo:(i + 1) * lo, :].astype(BF16)
                out[i][lo:, :] = sums[2 * lo + i * hi:2 * lo + (i + 1) * hi, :].astype(BF16)
            out[2][...] = sums[2 * ff:, :].astype(BF16)

    if outs:
        @pl.when(step == pl.num_programs(0) - 1)
        def _():
            end = tab_ref[b_at + step + 1] - 1
            lax.fori_loop(0, n_grp, lambda q, _: (scatter(end, q), 0)[1], 0)
            chunk = stage_f.shape[1]
            flights = {}
            n = 0
            for (o, _), out in zip(reversed(outs), [v for v in (du_outs, y_outs) if v]):
                for s in range(N_SRC):
                    wide = s == 0 or p_f32
                    stage = stage_f if wide else stage_b
                    for c in range(n_blk // chunk):
                        key = (wide, n % 2)
                        if key in flights:
                            flights.pop(key).wait()
                        for j, (cc, w) in enumerate(cols):
                            rows = pl.ds(PITCH * (s * n_blk + c * chunk) + o + j, chunk, stride=PITCH)
                            stage[n % 2, :, cc:cc + w] = acc[rows, 0:w].astype(stage.dtype)
                        flights[key] = pltpu.make_async_copy(
                            stage.at[n % 2], out[s].at[pl.ds(c * chunk, chunk), :], out_sem.at[2 * wide + n % 2])
                        flights[key].start()
                        n += 1
            for copy in flights.values():
                copy.wait()


def run_experts(tabs, lists, layer, half, x, mix, dy, mix_back, weights, prev, finals, fwd, own, p_f32=False):
    tab, where, width = tabs
    idx, gates, list_len = lists
    bwd = dy is not None
    wg, wu, wd = weights
    n_blk, d = x[0].shape
    n_layers, n_local, ff, _ = wd.shape
    n_exp = n_local // 2
    row_id = half * n_layers + layer
    at0 = row_id * width
    e_at = at0 + where[0]

    whole = pl.BlockSpec((n_blk, d), lambda e, *_: (0, 0), pipeline_mode=pl.Buffered(1))
    square = pl.BlockSpec((d, d), lambda e, *_: (0, 0), pipeline_mode=pl.Buffered(1))
    anyspec = pl.BlockSpec(memory_space=pl.ANY)
    weight = pl.BlockSpec((1, 1, ff, d), lambda e, tab: (layer, tab[e_at + e], 0, 0))
    partial = pl.BlockSpec((1, 3 * ff, d), lambda e, *_: (e, 0, 0))

    operands = [idx, gates, *x, mix]
    in_specs = [anyspec, anyspec] + [whole] * N_SRC + [square]
    if bwd:
        operands += list(dy)
        in_specs += [whole] * N_SRC
    if mix_back is not None:
        operands.append(mix_back)
        in_specs.append(square)
    operands += [wg, wu, wd]
    in_specs += [weight] * 3
    out_shape, out_specs, aliases = [], [], {}
    for use in (fwd, bwd and own):
        if use:
            out_shape += [jax.ShapeDtypeStruct((n_blk, d), F32 if s == 0 or p_f32 else BF16) for s in range(N_SRC)]
            out_specs += [anyspec] * N_SRC
    if bwd and own:
        out_shape.append(jax.ShapeDtypeStruct((n_exp, 3 * ff, d), F32))
        out_specs.append(partial)
    if bwd and not own:
        operands.append(prev)
        in_specs.append(partial)
        for i, f in enumerate(finals or ()):
            aliases[1 + len(operands)] = i
            operands.append(f)
            in_specs.append(anyspec)
        out_shape += [jax.ShapeDtypeStruct((n_layers, n_local, ff, d), BF16)] * 3
        out_specs += [weight] * 3
        out_shape.append(jax.ShapeDtypeStruct((n_exp, 3, ff, d), BF16))
        out_specs.append(pl.BlockSpec((1, 3, ff, d), lambda e, *_: (e, 0, 0, 0)))
    table = pltpu.VMEM((PITCH * N_SRC * n_blk + 512, LANES), F32)
    rows = pltpu.VMEM((HALF * ROWS, LANES), F32)
    mid = lambda n, dt: pltpu.VMEM((ROWS, n), dt)
    scratch = [table] * (1 + own) + [rows] * (1 + bwd) + [rows] * (fwd + (bwd and own))
    scratch += [pltpu.VMEM((2 * ff, d), BF16)] + [mid(d, BF16)] * (1 + bwd) + [mid(2 * ff, F32)]
    scratch += [mid(ff, F32)] * bwd + [mid(ff, BF16)] + [mid(2 * ff, BF16)] * bwd
    if bwd and not own:
        scratch.append(pltpu.VMEM((3 * ff, d), F32))
    n_list = N_SRC * (list_len + n_exp * GRP) + 64
    scratch += [pltpu.SMEM((n_list,), I32), pltpu.SMEM((n_list,), F32), pltpu.SemaphoreType.DMA((2,))]
    if own:
        scratch += [pltpu.VMEM((2, 256, d), F32), pltpu.VMEM((2, 256, d), BF16), pltpu.SemaphoreType.DMA((4,))]
    passes = 2 + fwd + bwd * (4 + 2 * own)
    flops = 2 * d * ff * passes * n_blk * N_SRC * 2
    cfg = (fwd, bwd, own, mix_back is not None, n_blk, d, ff, where, at0, row_id * N_SRC * list_len, list_len, n_exp,
           p_f32, len(aliases))
    return pl.pallas_call(
        functools.partial(expert_kernel, cfg),
        out_shape=out_shape,
        grid_spec=pltpu.PrefetchScalarGridSpec(
            num_scalar_prefetch=1, grid=(n_exp,), in_specs=in_specs, out_specs=out_specs, scratch_shapes=scratch),
        input_output_aliases=aliases,
        compiler_params=pltpu.CompilerParams(dimension_semantics=("arbitrary",), vmem_limit_bytes=VMEM_LIMIT),
        cost_estimate=pl.CostEstimate(flops=flops, bytes_accessed=3 * 2 * n_exp * d * ff, transcendentals=0),
        name=f"experts_{'f' if fwd else ''}{'b' if bwd else ''}_{'own' if own else 'other'}_{layer}",
    )(tab, *operands)


def place_kernel(tab_ref, got_ref, *refs):
    for i, out in enumerate(refs[3:]):
        out[0, 0] = got_ref[0, i]


def place(tabs, layer, got, finals):
    partner, width = tabs
    n_exp, _, ff, d = got.shape
    at = layer * n_exp
    final = pl.BlockSpec((1, 1, ff, d), lambda e, tab: (layer, tab[at + e], 0, 0))
    return pl.pallas_call(
        place_kernel,
        out_shape=[jax.ShapeDtypeStruct(f.shape, f.dtype) for f in finals],
        grid_spec=pltpu.PrefetchScalarGridSpec(
            num_scalar_prefetch=1, grid=(n_exp,),
            in_specs=[pl.BlockSpec((1, 3, ff, d), lambda e, *_: (e, 0, 0, 0))] + [pl.BlockSpec(memory_space=pl.ANY)] * 3,
            out_specs=[final] * 3),
        input_output_aliases={2: 0, 3: 1, 4: 2},
        compiler_params=pltpu.CompilerParams(dimension_semantics=("arbitrary",)),
        cost_estimate=pl.CostEstimate(flops=0, bytes_accessed=4 * got.size, transcendentals=0),
        name=f"place_{layer}",
    )(partner, got, *finals)


def peer(rel):
    return {name: (lax.axis_index(name) + ((rel >> bit) & 1)) % 2 for bit, name in enumerate(("ep", "core", "x"))}


def meet(rels):
    barrier = pltpu.get_barrier_semaphore()
    for rel in rels:
        pl.semaphore_signal(barrier, inc=1, device_id=peer(rel), device_id_type=MESH)
    pl.semaphore_wait(barrier, len(rels))


def share_kernel(n_rel, mine_ref, all_ref, send_sem, recv_sem):
    meet(range(1, n_rel))
    copies = [pltpu.make_async_remote_copy(
        src_ref=mine_ref, dst_ref=all_ref.at[rel], send_sem=send_sem.at[rel], recv_sem=recv_sem.at[rel],
        device_id=peer(rel), device_id_type=MESH) for rel in range(1, n_rel)]
    for copy in copies:
        copy.start()
    all_ref[0] = mine_ref[...]
    for copy in copies:
        copy.wait()


def share(mine, n_rel):
    return pl.pallas_call(
        functools.partial(share_kernel, n_rel),
        out_shape=jax.ShapeDtypeStruct((n_rel,) + mine.shape, mine.dtype),
        in_specs=[pl.BlockSpec(memory_space=pltpu.VMEM)],
        out_specs=pl.BlockSpec(memory_space=pltpu.VMEM),
        scratch_shapes=[pltpu.SemaphoreType.DMA((n_rel,)), pltpu.SemaphoreType.DMA((n_rel,))],
        compiler_params=pltpu.CompilerParams(collective_id=0, has_side_effects=True),
        cost_estimate=pl.CostEstimate(flops=10 ** 7, bytes_accessed=mine.size * 4 * n_rel, transcendentals=0),
        name="share_lists",
    )(mine)


Y, CORE = 1, 2


def sum_kernel(n_chunk, p_own, p_y, p_core, p_diag, o_own, o_y, o_core, o_diag,
               mine, got, s_buf, r_buf, y_buf, load_sem, d2d_send, d2d_recv, ys_send, ys_recv,
               yg_send, yg_recv, cg_send, cg_recv, fg_send, fg_recv, put_sem):
    rows = p_own.shape[0] // n_chunk
    cut = [pl.ds(k * rows, rows) for k in range(n_chunk)]
    loads = [[pltpu.make_async_copy(src.at[cut[k]], mine.at[i, cut[k]], load_sem.at[i, k]) for k in range(n_chunk)]
             for i, src in enumerate((p_y, p_own))]
    for i in range(2):
        for k in range(n_chunk):
            loads[i][k].start()
    meet((Y, CORE))

    def remote(src, dst, send, recv, rel):
        return pltpu.make_async_remote_copy(src_ref=src, dst_ref=dst, send_sem=send, recv_sem=recv,
                                            device_id=peer(rel), device_id_type=MESH)

    d2d = [[remote(src.at[cut[k]], got.at[i, cut[k]], d2d_send.at[i, k], d2d_recv.at[i, k], CORE)
            for k in range(n_chunk)] for i, src in enumerate((p_diag, p_core))]
    for i in range(2):
        for k in range(n_chunk):
            d2d[i][k].start()
    over = [remote(s_buf.at[cut[k]], r_buf.at[cut[k]], ys_send.at[k], ys_recv.at[k], Y) for k in range(n_chunk)]
    for k in range(n_chunk):
        loads[0][k].wait()
        d2d[0][k].wait_recv()
        s_buf[cut[k], :] = (mine[0, cut[k], :] + got[0, cut[k], :]).astype(BF16)
        over[k].start()
    to_y = [remote(y_buf.at[cut[k]], o_y.at[cut[k]], yg_send.at[k], yg_recv.at[k], Y) for k in range(n_chunk)]
    to_core = [remote(y_buf.at[cut[k]], o_core.at[cut[k]], cg_send.at[k], cg_recv.at[k], CORE) for k in range(n_chunk)]
    puts = [pltpu.make_async_copy(y_buf.at[cut[k]], o_own.at[cut[k]], put_sem.at[k]) for k in range(n_chunk)]
    for k in range(n_chunk):
        loads[1][k].wait()
        d2d[1][k].wait_recv()
        over[k].wait_recv()
        total = mine[1, cut[k], :] + got[1, cut[k], :] + r_buf[cut[k], :].astype(F32)
        y_buf[cut[k], :] = total.astype(BF16)
        to_y[k].start()
        to_core[k].start()
        puts[k].start()
    on = [remote(o_y.at[cut[k]], o_diag.at[cut[k]], fg_send.at[k], fg_recv.at[k], CORE) for k in range(n_chunk)]
    for k in range(n_chunk):
        to_y[k].wait_recv()
        on[k].start()
    for k in range(n_chunk):
        for i in range(2):
            d2d[i][k].wait_send()
        over[k].wait_send()
        to_y[k].wait_send()
        to_core[k].wait()
        puts[k].wait()
        on[k].wait()


def sum_blocks(parts, n_chunk=4):
    n_blk, d = parts[0].shape
    anyspec = pl.BlockSpec(memory_space=pl.ANY)
    sem = lambda *s: pltpu.SemaphoreType.DMA(s)
    n = n_chunk
    return pl.pallas_call(
        functools.partial(sum_kernel, n_chunk),
        out_shape=[jax.ShapeDtypeStruct((n_blk, d), BF16)] * N_SRC,
        in_specs=[anyspec] * N_SRC,
        out_specs=[anyspec] * N_SRC,
        scratch_shapes=[pltpu.VMEM((2, n_blk, d), F32), pltpu.VMEM((2, n_blk, d), F32), pltpu.VMEM((n_blk, d), BF16),
                        pltpu.VMEM((n_blk, d), BF16), pltpu.VMEM((n_blk, d), BF16), sem(2, n), sem(2, n), sem(2, n),
                        sem(n), sem(n), sem(n), sem(n), sem(n), sem(n), sem(n), sem(n), sem(n)],
        compiler_params=pltpu.CompilerParams(collective_id=1, has_side_effects=True, vmem_limit_bytes=VMEM_LIMIT),
        cost_estimate=pl.CostEstimate(flops=10 ** 8, bytes_accessed=n_blk * d * 40, transcendentals=0),
        name="sum_blocks",
    )(*parts)


def solution(mesh):
    ep_size, dp_size = mesh.shape['ep'], mesh.shape['dp']
    sub = Mesh(mesh.devices.reshape(ep_size, dp_size // 2, 2), ('ep', 'x', 'core'))
    tok_axes = ('x', 'core', 'ep')
    tok_spec = P(tok_axes, None)
    route_spec = P(None, tok_axes, None)
    whole_spec = P(None, None, None)
    expert_spec = P(None, 'ep', None, None)
    flip = [(0, 1), (1, 0)]
    move = lambda v, axis: lax.ppermute(v, axis, flip)

    def device_step(tokens, d_out, expert_ids, gate_vals, w_mix, w_gate, w_up, w_down):
        n_layers = w_mix.shape[0]
        n_tok, d = tokens.shape
        top = expert_ids.shape[2]
        n_local, ff = w_gate.shape[1], w_gate.shape[3]
        n_exp = n_local * ep_size
        n = n_tok * top
        n_rel = 2 * N_SRC
        cap = cdiv(CAP_FACTOR * n, n_exp)
        per_tile = ROWS // GRP
        max_groups = cdiv(N_SRC * cdiv(cap, GRP), per_tile) * per_tile
        ic, ie = lax.axis_index('core'), lax.axis_index('ep')
        weights = (jnp.swapaxes(w_gate, 2, 3), jnp.swapaxes(w_up, 2, 3), w_down)

        def spread(own):
            far = move(own, 'ep')
            return [own, far, move(own, 'core'), move(far, 'core')]

        def across(blocks):
            a, b = move(blocks[0], 'x'), move(blocks[1], 'x')
            return [a, b, move(a, 'core'), move(b, 'core')]

        x0 = spread(tokens)
        lists = [sorted_list(expert_ids[l], gate_vals[l]) for l in range(n_layers)]
        counts = jnp.sum((expert_ids.reshape(n_layers, n, 1) == jnp.arange(n_exp, dtype=I32)).astype(F32), axis=1)
        packed = jnp.concatenate([jnp.concatenate([v[0] for v in lists] + [v[1] for v in lists]).reshape(-1, LANES),
                                  jnp.pad(counts, ((0, 8 - n_layers), (0, LANES - n_exp)))], axis=0)
        packed = share(packed, n_rel)
        n_rows = n // LANES
        cnt = packed[:, 2 * n_layers * n_rows:2 * n_layers * n_rows + n_layers, :n_exp].astype(I32)
        tab, where, width = scalar_tables(cnt, ie * n_local, n_local, ic, n, max_groups)
        halves = lambda v: v.reshape(2, N_SRC, n_layers, n_rows, LANES).transpose(0, 2, 1, 3, 4).reshape(-1)
        block = jnp.arange(n_rel, dtype=I32)[:, None, None] % N_SRC * n_tok
        idx = halves((packed[:, :n_layers * n_rows].astype(I32) + block) * PITCH)
        gates = halves(packed[:, n_layers * n_rows:2 * n_layers * n_rows])
        tabs = (tab, where, width)
        lists = (idx, gates, n)
        mine = jnp.concatenate([lax.slice_in_dim(tab, l * width, l * width + n_local // 2) for l in range(n_layers)])
        partner = (move(mine, 'core'), None)

        part = run_experts(tabs, lists, 0, 0, x0, w_mix[0], None, None, weights, None, None, True, True, p_f32=True)
        dy1 = spread(d_out)
        x1 = sum_blocks(part)
        x1o, dy1o, x0o = across(x1), across(dy1), across(x0)
        out = run_experts(tabs, lists, 1, 0, x1, w_mix[1], dy1, None, weights, None, None, True, True)
        y_part, du_part, g1 = out[:4], out[4:8], out[8]
        def sum_far(p):
            got = [lax.ppermute(p[1], 'ep', flip), lax.ppermute(p[2], 'core', flip),
                   lax.ppermute(p[3], ('ep', 'core'), [(0, 3), (1, 2), (2, 1), (3, 0)])]
            return sum([g.astype(F32) for g in got], p[0]).astype(BF16)

        du1 = sum_far(du_part)
        *finals, sent1 = run_experts(tabs, lists, 1, 1, x1o, w_mix[1], dy1o, None, weights, g1, None, False, False)
        du1 = spread(du1)
        du1o = across(du1)
        got1 = move(sent1, 'core')
        out = run_experts(tabs, lists, 0, 0, x0, w_mix[0], du1, w_mix[1], weights, None, None, False, True)
        du_part, g0 = out[:4], out[4]
        y1 = sum_far(y_part)
        du0 = sum_far(du_part)
        *finals, sent0 = run_experts(tabs, lists, 0, 1, x0o, w_mix[0], du1o, w_mix[1], weights, g0, finals, False, False)
        got0 = move(sent0, 'core')
        finals = place(partner, 1, got1, finals)

        tx = lambda x, du: jnp.einsum('td,te->de', x, du, preferred_element_type=F32)
        g_mix1 = tx(jnp.concatenate(list(x1) + list(x1o)), jnp.concatenate(list(du1) + list(du1o)))
        dx0 = (du0.astype(F32) + jnp.einsum('te,de->td', du0, w_mix[0], preferred_element_type=F32)).astype(BF16)
        g_mix0 = lax.psum(tx(tokens, du0).astype(BF16), tok_axes)
        g_mix = jnp.stack([g_mix0, g_mix1.astype(BF16)])
        finals = place(partner, 0, got0, finals)
        return (y1, dx0, g_mix, jnp.swapaxes(finals[0], 2, 3), jnp.swapaxes(finals[1], 2, 3), finals[2])

    return jax.shard_map(device_step, mesh=sub,
                         in_specs=(tok_spec, tok_spec, route_spec, route_spec, whole_spec,
                                   expert_spec, expert_spec, expert_spec),
                         out_specs=(tok_spec, tok_spec, whole_spec, expert_spec, expert_spec, expert_spec),
                         check_vma=False)
```

time: 4780 us -> 958 us (0.20)
  waiting for transfers between devices: 1790 us -> 126 us
  local copies, waits for them, and re-layouts: 1520 us -> 171 us
  Pallas kernels: 0 us -> 577 us
  matrix products: 504 us -> 13.4 us
  blocking collectives: 488 us -> 0 us
  other arithmetic: 368 us -> 36.9 us
    gather x26 -> x0, local copies, waits for them, and re-layouts: 1090 us -> none  [the longest x4 272 us: layer_backward(): g_dy[src_copy]]
    psum x2 -> x1, waiting for transfers between devices: 1040 us -> 30.5 us  [device_step(): g_mix0 = lax.psum(tx(tokens, du0).astype(BF16), tok_axes)]
    all_to_all x6 -> x0, waiting for transfers between devices: 753 us -> none  [the longest x1 215 us: layer_backward(): recv_grad = lax.all_to_all(send_grad, 'ep', 0, 0, tiled=True)]
    pallas_call x0 -> x9, Pallas kernels: none -> 577 us  [the longest x5 465 us: run_experts(): pl.pallas_call(functools.partial(expert_kernel, cfg), out_shape=out_shape...]
    dot_general x24 -> x3, matrix products: 504 us -> 13.4 us  [the longest x2 12.7 us: device_step(): jnp.einsum('td,te->de', x, du, preferred_element_type=F32)]
    all_to_all x2 -> x0, blocking collectives: 488 us -> none  [the longest x1 247 us: layer_forward(): recv_buf = lax.all_to_all(send_buf, 'ep', 0, 0, tiled=True)]
    select_n x10 -> x0, local copies, waits for them, and re-layouts: 154 us -> none  [the longest x4 76.8 us: layer_forward(): send_buf = jnp.where(is_valid[:, :, None], u_act[src_copy // top_k], 0)]
    scatter-add x2 -> x0, other arithmetic: 114 us -> none  [route_tables(): counts = jnp.bincount(flat_ids, length=n_experts)]
  transfers between devices with their start and end apart: 8 -> 38, of which waited for: 7 -> 9; matrix products, arithmetic and copies ran while one was open for 19% -> 22% of each run, Pallas kernels for 0% -> 58%
where the time goes in v2:
time: 958 us; the launch traced here: 964 us
  Pallas kernels  577 us (60%)
  local copies, waits for them, and re-layouts  171 us (18%)
  waiting for transfers between devices  126 us (13%)
  other arithmetic  36.9 us (4%)
  starting transfers between devices  24.7 us (3%)
  between operations  15.1 us (2%)
  matrix products  13.4 us (1%)
    pallas_call x5, Pallas kernels, run_experts(): pl.pallas_call(functools.partial(expert_kernel, cfg), out_shape=out_shape...  465 us
    ppermute x25, local copies, waits for them, and re-layouts, solution(): move = lambda v, axis: lax.ppermute(v, axis, flip)  54.3 us
    pallas_call x1, Pallas kernels, sum_blocks(): pl.pallas_call(functools.partial(sum_kernel, n_chunk), out_shape=[jax.Sha...  49.9 us
    ppermute x3, waiting for transfers between devices, sum_far(): lax.ppermute(p[1], 'ep', flip)  39.4 us
    pallas_call x2, Pallas kernels, place(): pl.pallas_call(place_kernel, out_shape=[jax.ShapeDtypeStruct(f.shape, f.d...  35 us
    ppermute x3, waiting for transfers between devices, sum_far(): lax.ppermute(p[3], ('ep', 'core'), [(0, 3), (1, 2), (2, 1), (3, 0)])  33.7 us
    unnamed x81, local copies, waits for them, and re-layouts  32.7 us
    psum x1, waiting for transfers between devices, device_step(): g_mix0 = lax.psum(tx(tokens, du0).astype(BF16), tok_axes)  30.5 us
  transfers between devices with their start and end apart: 38, of which 9 were waited for; matrix products, arithmetic and copies ran while one was open for 22% of the time, Pallas kernels for 58%

profile of v2, /device:TPU:0, one launch (start us, length us, event | category | flops | bytes accessed | tf_op | source)
XLA Modules:
  0.0 964.0 jit_solution(16000641623780499015)
XLA Ops:
  20.4 6.9 sort.46
  28.7 6.9 sort.47
  36.3 27.6 %share_lists.1 = f32[8,264,128]{2,1,0:T(8,128)} custom-call(f32[264,128]{1,0:T(8,128)} %copy-done.22), custom_call_target="tpu_custom_call" | custom-call | flops 10000000 | bytes 1081344 | tf_op jit(solution)/shard_map/share_lists/pallas_call | solution.py:453
  127.4 54.4 %experts_f_own_0.1 = (f32[1024,448]{1,0:T(8,128)}, f32[1024,448]{1,0:T(8,128)}, f32[1024,448]{1,0:T(8,128)}, f32[1024,448]{1,0:T(8,128)}) custom-call(s32[13196]{0:T(1024)} %reshape.215.refs_0_, s32[131072]{0:T(1024)} %bitcast.136, f32[131072]{0:T(1024)} %bitcast.131, bf16[1024,448]{1,0:T(8,128)(2,1)} %copy.237.refs_3_, bf16[1024,448]{1,0:T(8,128)(2,1)} %copy.238.refs_4_, ...), custom_call_target="tpu_custom_call" | custom-call | flops 7046430720 | bytes 13762560 | tf_op jit(solution)/shard_map/experts_f_own_0/pallas_call | solution.py:393
  181.8 49.9 %sum_blocks.1 = (bf16[1024,448]{1,0:T(8,128)(2,1)}, bf16[1024,448]{1,0:T(8,128)(2,1)}, bf16[1024,448]{1,0:T(8,128)(2,1)}, bf16[1024,448]{1,0:T(8,128)(2,1)}) custom-call(f32[1024,448]{1,0:T(8,128)} %get-tuple-element.54.p_own, f32[1024,448]{1,0:T(8,128)} %get-tuple-element.55.p_y, f32[1024,448]{1,0:T(8,128)} %get-tuple-element.56.p_core, ...), custom_call_target="tpu_custom_call" | custom-call | flops 100000000 | bytes 18350080 | tf_op jit(solution)/shard_map/sum_blocks/pallas_call | solution.py:526
  234.0 125.4 %experts_fb_own_1.1 = (f32[1024,448]{1,0:T(8,128)}, bf16[1024,448]{1,0:T(8,128)(2,1)}, bf16[1024,448]{1,0:T(8,128)(2,1)}, bf16[1024,448]{1,0:T(8,128)(2,1)}, f32...) custom-call(s32[13196]{0:T(1024)} %reshape.215.refs_0_, ...), custom_call_target="tpu_custom_call" | custom-call | flops 21139292160 | bytes 13762560 | tf_op jit(solution)/shard_map/experts_fb_own_1/pallas_call | solution.py:393
  371.1 12.6 %collective-permute-done.11 = bf16[1024,448]{0,1:T(8,128)(2,1)} collective-permute-done((bf16[1024,448]{0,1:T(8,128)(2,1)}, bf16[1024,448]{0,1:T(8,128)(2,1)}, u32[]{:S(2)}, u32[]{:S(2)}) %collective-permute-start.11) | collective-permute-done | bytes 917536 | tf_op jit(solution)/shard_map/ppermute | solution.py:599
  387.0 7.5 collective-permute-done.9
  401.9 3.4 constant_dynamic-update-slice_fusion.20
  407.3 3.9 collective-permute-done.19
  411.2 18.4 %collective-permute-done.18 = bf16[1024,448]{0,1:T(8,128)(2,1)} collective-permute-done((bf16[1024,448]{0,1:T(8,128)(2,1)}, bf16[1024,448]{0,1:T(8,128)(2,1)}, u32[]{:S(2)}, u32[]{:S(2)}) %collective-permute-start.18) | collective-permute-done | bytes 917536 | tf_op jit(solution)/shard_map/ppermute | solution.py:549
  459.4 84.2 %experts_b_other_1.1 = (bf16[2,32,320,448]{3,2,1,0:T(8,128)(2,1)}, bf16[2,32,320,448]{3,2,1,0:T(8,128)(2,1)}, bf16[2,32,320,448]{3,2,1,0:T(8,128)(2,1)}, bf16[16,3,320,448]{3,2,1,0:T(8,128)(2,1)}) custom-call(s32[13196]{0:T(1024)} %reshape.215.refs_0_, s32[131072]{0:T(1024)} %bitcast.138, f32[131072]{0:T(1024)} %bitcast.133, ...), custom_call_target="tpu_custom_call" | custom-call | flops 14092861440 | bytes 13762560 | tf_op jit(solution)/shard_map/experts_b_other_1/pallas_call | solution.py:393
  556.7 112.6 %experts_b_own_0.1 = (f32[1024,448]{1,0:T(8,128)}, bf16[1024,448]{1,0:T(8,128)(2,1)}, bf16[1024,448]{1,0:T(8,128)(2,1)}, bf16[1024,448]{1,0:T(8,128)(2,1)}, f32[16,960,448]{2,1,0:T(8,128)}) custom-call(s32[13196]{0:T(1024)} %reshape.215.refs_0_, s32[131072]{0:T(1024)} %bitcast.139, f32[131072]{0:T(1024)} %bitcast.134, bf16[1024,448]{1,0:T(8,128)(2,1)} %copy.237.refs_3_, ...), custom_call_target="tpu_custom_call" | custom-call | flops 18790481920 | bytes 13762560 | tf_op jit(solution)/shard_map/experts_b_own_0/pallas_call | solution.py:393
  670.6 87.9 %experts_b_other_0.1 = (bf16[2,32,320,448]{3,2,1,0:T(8,128)(2,1)}, bf16[2,32,320,448]{3,2,1,0:T(8,128)(2,1)}, bf16[2,32,320,448]{3,2,1,0:T(8,128)(2,1)}, bf16[16,3,320,448]{3,2,1,0:T(8,128)(2,1)}) custom-call(s32[13196]{0:T(1024)} %reshape.215.refs_0_, s32[131072]{0:T(1024)} %bitcast.140, ...), custom_call_target="tpu_custom_call", output_to_operand_aliasing={{0}: (17, {}), {1}: (18, {}), {2}: (19, {})} | custom-call | flops 14092861440 | bytes 13762560 | tf_op jit(solution)/shard_map/experts_b_other_0/pallas_call | solution.py:393
  771.4 3.2 copy-done.24
  774.6 10.5 %collective-permute-done.8 = bf16[1024,448]{0,1:T(8,128)(2,1)} collective-permute-done((bf16[1024,448]{0,1:T(8,128)(2,1)}, bf16[1024,448]{0,1:T(8,128)(2,1)}, u32[]{:S(2)}, u32[]{:S(2)}) %collective-permute-start.8) | collective-permute-done | bytes 917536 | tf_op jit(solution)/shard_map/ppermute | solution.py:599
  788.9 16.5 %collective-permute-done.6 = bf16[1024,448]{0,1:T(8,128)(2,1)} collective-permute-done((bf16[1024,448]{0,1:T(8,128)(2,1)}, bf16[1024,448]{0,1:T(8,128)(2,1)}, u32[]{:S(2)}, u32[]{:S(2)}) %collective-permute-start.6) | collective-permute-done | bytes 917536 | tf_op jit(solution)/shard_map/ppermute | solution.py:598
  807.7 3.7 add_convert_fusion.3
  837.0 10.6 %collective-permute-done.17 = bf16[1024,448]{0,1:T(8,128)(2,1)S(1)} collective-permute-done((bf16[1024,448]{0,1:T(8,128)(2,1)}, bf16[1024,448]{0,1:T(8,128)(2,1)S(1)}, u32[]{:S(2)}, u32[]{:S(2)}) %collective-permute-start.17) | collective-permute-done | bytes 917536 | tf_op jit(solution)/shard_map/ppermute | solution.py:599
  851.4 15.4 %collective-permute-done.15 = bf16[1024,448]{0,1:T(8,128)(2,1)} collective-permute-done((bf16[1024,448]{0,1:T(8,128)(2,1)}, bf16[1024,448]{0,1:T(8,128)(2,1)}, u32[]{:S(2)}, u32[]{:S(2)}) %collective-permute-start.15) | collective-permute-done | bytes 917536 | tf_op jit(solution)/shard_map/ppermute | solution.py:598
  876.4 9.9 %fusion.1 = bf16[1,448,448]{1,2,0:T(8,128)(2,1)S(1)} fusion(bf16[8192,448]{1,0:T(8,128)(2,1)} %constant_dynamic-update-slice_fusion.5, bf16[8192,448]{1,0:T(8,128)(2,1)} %constant_dynamic-update-slice_fusion.13), kind=kOutput, calls=%fused_computation.9 | convolution fusion | flops 3288535040 | bytes 15081472 | tf_op jit(solution)/shard_map/td,te->de/dot_general | solution.py:615
  888.4 30.5 %all-reduce.3.cloned.1.call-done = bf16[1,448,448]{1,2,0:T(8,128)(2,1)} async-done(((bf16[1,448,448]{1,2,0:T(8,128)(2,1)}), bf16[1,448,448]{1,2,0:T(8,128)(2,1)}) %all-reduce.3.cloned.1.call-update) | async-done | bytes 401424 | tf_op jit(solution)/shard_map/psum | solution.py:618
  921.7 17.5 %place_1.1 = (bf16[2,32,320,448]{3,2,1,0:T(8,128)(2,1)}, bf16[2,32,320,448]{3,2,1,0:T(8,128)(2,1)}, bf16[2,32,320,448]{3,2,1,0:T(8,128)(2,1)}) custom-call(s32[32]{0:T(128)} %copy-done.29, bf16[16,3,320,448]{3,2,1,0:T(8,128)(2,1)} %collective-permute-done.36.got_ref, ...), custom_call_target="tpu_custom_call", output_to_operand_aliasing={{0}: (2, {}), {1}: (3, {}), {2}: (4, {})} | custom-call | bytes 27525120 | tf_op jit(solution)/shard_map/place_1/pallas_call | solution.py:415
  939.2 17.5 %place_0.1 = (bf16[2,32,320,448]{3,2,1,0:T(8,128)(2,1)}, bf16[2,32,320,448]{3,2,1,0:T(8,128)(2,1)}, bf16[2,32,320,448]{3,2,1,0:T(8,128)(2,1)}) custom-call(s32[32]{0:T(128)} %copy-done.29, bf16[16,3,320,448]{3,2,1,0:T(8,128)(2,1)} %collective-permute-done.35.got_ref, ...), custom_call_target="tpu_custom_call", output_to_operand_aliasing={{0}: (2, {}), {1}: (3, {}), {2}: (4, {})} | custom-call | bytes 27525120 | tf_op jit(solution)/shard_map/place_0/pallas_call | solution.py:415
  (310 shorter events, 212.0 us)
Async XLA Ops:
  7.2 911.6 %all-reduce.3.cloned.1.call-start = ((), (), s32[]{:S(2)}) async-start(), calls=%async_computation | async-start | bytes 917504 | tf_op jit(solution)/shard_map/psum | solution.py:618
  7.2 111.4 %collective-permute-start.4 = (bf16[1024,448]{0,1:T(8,128)(2,1)}, bf16[1024,448]{0,1:T(8,128)(2,1)}, u32[]{:S(2)}, u32[]{:S(2)}) collective-permute-start(bf16[1024,448]{0,1:T(8,128)(2,1)} %param.9), channel_id=1, source_target_pairs={{0,1},{1,0},{2,3},{3,2},{4,5},{5,4},{6,7},{7,6}} | collective-permute-start | bytes 2752520 | tf_op jit(solution)/shard_map/ppermute | solution.py:549
  8.1 104.6 %collective-permute-start.3 = (bf16[1024,448]{0,1:T(8,128)(2,1)}, bf16[1024,448]{0,1:T(8,128)(2,1)}, u32[]{:S(2)}, u32[]{:S(2)}) collective-permute-start(bf16[1024,448]{0,1:T(8,128)(2,1)} %param.9), channel_id=1, source_target_pairs={{0,4},{4,0},{1,5},{5,1},{2,6},{6,2},{3,7},{7,3}} | collective-permute-start | bytes 2752520 | tf_op jit(solution)/shard_map/ppermute | solution.py:549
  10.6 111.7 %collective-permute-start.31 = (bf16[1024,448]{0,1:T(8,128)(2,1)}, bf16[1024,448]{0,1:T(8,128)(2,1)}, u32[]{:S(2)}, u32[]{:S(2)}) collective-permute-start(bf16[1024,448]{0,1:T(8,128)(2,1)} %param.9), channel_id=1, source_target_pairs={{0,2},{2,0},{1,3},{3,1},{4,6},{6,4},{5,7},{7,5}} | collective-permute-start | bytes 2752520 | tf_op jit(solution)/shard_map/ppermute | solution.py:549
  12.1 110.8 %collective-permute-start.1 = (bf16[1024,448]{0,1:T(8,128)(2,1)}, bf16[1024,448]{0,1:T(8,128)(2,1)}, u32[]{:S(2)}, u32[]{:S(2)}) collective-permute-start(bf16[1024,448]{0,1:T(8,128)(2,1)} %param.8), channel_id=1, source_target_pairs={{0,1},{1,0},{2,3},{3,2},{4,5},{5,4},{6,7},{7,6}} | collective-permute-start | bytes 2752520 | tf_op jit(solution)/shard_map/ppermute | solution.py:549
  12.1 95.3 %collective-permute-start = (bf16[1024,448]{0,1:T(8,128)(2,1)}, bf16[1024,448]{0,1:T(8,128)(2,1)}, u32[]{:S(2)}, u32[]{:S(2)}) collective-permute-start(bf16[1024,448]{0,1:T(8,128)(2,1)} %param.8), channel_id=1, source_target_pairs={{0,4},{4,0},{1,5},{5,1},{2,6},{6,2},{3,7},{7,3}} | collective-permute-start | bytes 2752520 | tf_op jit(solution)/shard_map/ppermute | solution.py:549
  112.7 119.0 %collective-permute-start.5 = (bf16[1024,448]{0,1:T(8,128)(2,1)}, bf16[1024,448]{0,1:T(8,128)(2,1)}, u32[]{:S(2)}, u32[]{:S(2)}) collective-permute-start(bf16[1024,448]{0,1:T(8,128)(2,1)} %collective-permute-done.3), channel_id=1, source_target_pairs={{0,1},{1,0},{2,3},{3,2},{4,5},{5,4},{6,7},{7,6}} | collective-permute-start | bytes 2752520 | tf_op jit(solution)/shard_map/ppermute | solution.py:549
  118.6 247.6 %collective-permute-start.27 = (bf16[1024,448]{0,1:T(8,128)(2,1)S(1)}, bf16[1024,448]{0,1:T(8,128)(2,1)}, u32[]{:S(2)}, u32[]{:S(2)}) collective-permute-start(bf16[1024,448]{0,1:T(8,128)(2,1)S(1)} %copy-done.19), channel_id=1, source_target_pairs={{0,2},{2,0},{1,3},{3,1},{4,6},{6,4},{5,7},{7,5}} | collective-permute-start | bytes 2752520 | tf_op jit(solution)/shard_map/ppermute | solution.py:549
  122.3 246.0 %collective-permute-start.32 = (bf16[1024,448]{0,1:T(8,128)(2,1)}, bf16[1024,448]{0,1:T(8,128)(2,1)}, u32[]{:S(2)}, u32[]{:S(2)}) collective-permute-start(bf16[1024,448]{0,1:T(8,128)(2,1)} %collective-permute-done.3), channel_id=1, source_target_pairs={{0,2},{2,0},{1,3},{3,1},{4,6},{6,4},{5,7},{7,5}} | collective-permute-start | bytes 2752520 | tf_op jit(solution)/shard_map/ppermute | solution.py:549
  122.9 248.2 %collective-permute-start.33 = (bf16[1024,448]{0,1:T(8,128)(2,1)}, bf16[1024,448]{0,1:T(8,128)(2,1)}, u32[]{:S(2)}, u32[]{:S(2)}) collective-permute-start(bf16[1024,448]{0,1:T(8,128)(2,1)} %collective-permute-done.31), channel_id=1, source_target_pairs={{0,1},{1,0},{2,3},{3,2},{4,5},{5,4},{6,7},{7,6}} | collective-permute-start | bytes 2752520 | tf_op jit(solution)/shard_map/ppermute | solution.py:549
  386.4 43.2 %collective-permute-start.18 = (bf16[1024,448]{0,1:T(8,128)(2,1)}, bf16[1024,448]{0,1:T(8,128)(2,1)}, u32[]{:S(2)}, u32[]{:S(2)}) collective-permute-start(bf16[1024,448]{0,1:T(8,128)(2,1)} %copy.273), channel_id=1, source_target_pairs={{0,2},{2,0},{1,3},{3,1},{4,6},{6,4},{5,7},{7,5}} | collective-permute-start | bytes 2752520 | tf_op jit(solution)/shard_map/ppermute | solution.py:549
  405.3 46.1 %collective-permute-start.30 = (bf16[1024,448]{0,1:T(8,128)(2,1)}, bf16[1024,448]{0,1:T(8,128)(2,1)}, u32[]{:S(2)}, u32[]{:S(2)}) collective-permute-start(bf16[1024,448]{0,1:T(8,128)(2,1)} %collective-permute-done.28), channel_id=1, source_target_pairs={{0,1},{1,0},{2,3},{3,2},{4,5},{5,4},{6,7},{7,6}} | collective-permute-start | bytes 2752520 | tf_op jit(solution)/shard_map/ppermute | solution.py:549
  406.9 47.0 %collective-permute-start.12 = (bf16[1024,448]{0,1:T(8,128)(2,1)S(1)}, bf16[1024,448]{0,1:T(8,128)(2,1)S(1)}, u32[]{:S(2)}, u32[]{:S(2)}) collective-permute-start(bf16[1024,448]{0,1:T(8,128)(2,1)S(1)} %copy.257), channel_id=1, source_target_pairs={{0,4},{4,0},{1,5},{5,1},{2,6},{6,2},{3,7},{7,3}} | collective-permute-start | bytes 2752520 | tf_op jit(solution)/shard_map/ppermute | solution.py:549
  411.2 43.2 %collective-permute-start.21 = (bf16[1024,448]{0,1:T(8,128)(2,1)}, bf16[1024,448]{0,1:T(8,128)(2,1)}, u32[]{:S(2)}, u32[]{:S(2)}) collective-permute-start(bf16[1024,448]{0,1:T(8,128)(2,1)} %collective-permute-done.19), channel_id=1, source_target_pairs={{0,1},{1,0},{2,3},{3,2},{4,5},{5,4},{6,7},{7,6}} | collective-permute-start | bytes 2752520 | tf_op jit(solution)/shard_map/ppermute | solution.py:549
  451.4 95.8 %collective-permute-start.13 = (bf16[1024,448]{0,1:T(8,128)(2,1)S(1)}, bf16[1024,448]{0,1:T(8,128)(2,1)}, u32[]{:S(2)}, u32[]{:S(2)}) collective-permute-start(bf16[1024,448]{0,1:T(8,128)(2,1)S(1)} %copy.257), channel_id=1, source_target_pairs={{0,1},{1,0},{2,3},{3,2},{4,5},{5,4},{6,7},{7,6}} | collective-permute-start | bytes 2752520 | tf_op jit(solution)/shard_map/ppermute | solution.py:549
  453.9 95.6 %collective-permute-start.23 = (bf16[1024,448]{0,1:T(8,128)(2,1)S(1)}, bf16[1024,448]{0,1:T(8,128)(2,1)}, u32[]{:S(2)}, u32[]{:S(2)}) collective-permute-start(bf16[1024,448]{0,1:T(8,128)(2,1)S(1)} %collective-permute-done.12), channel_id=1, source_target_pairs={{0,2},{2,0},{1,3},{3,1},{4,6},{6,4},{5,7},{7,5}} | collective-permute-start | bytes 2752520 | tf_op jit(solution)/shard_map/ppermute | solution.py:549
  454.4 100.0 %collective-permute-start.14 = (bf16[1024,448]{0,1:T(8,128)(2,1)S(1)}, bf16[1024,448]{0,1:T(8,128)(2,1)}, u32[]{:S(2)}, u32[]{:S(2)}) collective-permute-start(bf16[1024,448]{0,1:T(8,128)(2,1)S(1)} %collective-permute-done.12), channel_id=1, source_target_pairs={{0,1},{1,0},{2,3},{3,2},{4,5},{5,4},{6,7},{7,6}} | collective-permute-start | bytes 2752520 | tf_op jit(solution)/shard_map/ppermute | solution.py:549
  458.9 93.3 %collective-permute-start.24 = (bf16[1024,448]{0,1:T(8,128)(2,1)}, bf16[1024,448]{0,1:T(8,128)(2,1)}, u32[]{:S(2)}, u32[]{:S(2)}) collective-permute-start(bf16[1024,448]{0,1:T(8,128)(2,1)} %collective-permute-done.22), channel_id=1, source_target_pairs={{0,1},{1,0},{2,3},{3,2},{4,5},{5,4},{6,7},{7,6}} | collective-permute-start | bytes 2752520 | tf_op jit(solution)/shard_map/ppermute | solution.py:549
  543.6 377.6 %collective-permute-start.36 = (bf16[16,3,320,448]{3,2,1,0:T(8,128)(2,1)}, bf16[16,3,320,448]{3,2,1,0:T(8,128)(2,1)}, u32[]{:S(2)}, u32[]{:S(2)}) collective-permute-start(bf16[16,3,320,448]{3,2,1,0:T(8,128)(2,1)} %get-tuple-element.80), channel_id=1, source_target_pairs={{0,1},{1,0},{2,3},{3,2},{4,5},{5,4},{6,7},{7,6}} | collective-permute-start | bytes 41287688 | tf_op jit(solution)/shard_map/ppermute | solution.py:549
  549.4 119.9 %collective-permute-start.25 = (bf16[1024,448]{0,1:T(8,128)(2,1)}, bf16[1024,448]{0,1:T(8,128)(2,1)S(1)}, u32[]{:S(2)}, u32[]{:S(2)}) collective-permute-start(bf16[1024,448]{0,1:T(8,128)(2,1)} %collective-permute-done.23), channel_id=1, source_target_pairs={{0,1},{1,0},{2,3},{3,2},{4,5},{5,4},{6,7},{7,6}} | collective-permute-start | bytes 2752520 | tf_op jit(solution)/shard_map/ppermute | solution.py:549
  758.6 180.6 %collective-permute-start.35 = (bf16[16,3,320,448]{3,2,1,0:T(8,128)(2,1)}, bf16[16,3,320,448]{3,2,1,0:T(8,128)(2,1)}, u32[]{:S(2)}, u32[]{:S(2)}) collective-permute-start(bf16[16,3,320,448]{3,2,1,0:T(8,128)(2,1)} %get-tuple-element.79), channel_id=1, source_target_pairs={{0,1},{1,0},{2,3},{3,2},{4,5},{5,4},{6,7},{7,6}} | collective-permute-start | bytes 41287688 | tf_op jit(solution)/shard_map/ppermute | solution.py:549
  766.0 39.5 %collective-permute-start.6 = (bf16[1024,448]{0,1:T(8,128)(2,1)}, bf16[1024,448]{0,1:T(8,128)(2,1)}, u32[]{:S(2)}, u32[]{:S(2)}) collective-permute-start(bf16[1024,448]{0,1:T(8,128)(2,1)} %copy.245), channel_id=1, source_target_pairs={{0,4},{4,0},{1,5},{5,1},{2,6},{6,2},{3,7},{7,3}} | collective-permute-start | bytes 2752520 | tf_op jit(solution)/shard_map/ppermute | solution.py:598
  825.3 41.5 %collective-permute-start.15 = (bf16[1024,448]{0,1:T(8,128)(2,1)}, bf16[1024,448]{0,1:T(8,128)(2,1)}, u32[]{:S(2)}, u32[]{:S(2)}) collective-permute-start(bf16[1024,448]{0,1:T(8,128)(2,1)} %copy.266), channel_id=1, source_target_pairs={{0,4},{4,0},{1,5},{5,1},{2,6},{6,2},{3,7},{7,3}} | collective-permute-start | bytes 2752520 | tf_op jit(solution)/shard_map/ppermute | solution.py:598
  848.5 72.7 %collective-permute-start.26 = (s32[32]{0:T(128)S(1)}, s32[32]{0:T(128)S(1)}, u32[]{:S(2)}, u32[]{:S(2)}) collective-permute-start(s32[32]{0:T(128)S(1)} %pad_add_fusion), channel_id=1, source_target_pairs={{0,1},{1,0},{2,3},{3,2},{4,5},{5,4},{6,7},{7,6}} | collective-permute-start | bytes 392 | tf_op jit(solution)/shard_map/ppermute | solution.py:549
  (45 other events, 1274.9 us)
Sparse Core Ops, SparseCore 0:
  875.5 43.2 all-reduce.2

commit v3 on v2

v3 whole, which is shorter than its diff:
```python
import functools

import jax
import jax.numpy as jnp
from jax import lax
from jax.experimental import pallas as pl
from jax.experimental.pallas import tpu as pltpu
from jax.sharding import Mesh, PartitionSpec as P

F32, BF16, I32 = jnp.float32, jnp.bfloat16, jnp.int32
MESH = pl.DeviceIdType.MESH
ROWS = 384
GRP = 8
PITCH = 8
HALF = 4
CAP_FACTOR = 3
LANES = 128
N_SRC = 4
Y, CORE, X = 1, 2, 4
VMEM_LIMIT = 62 * 1024 * 1024
PER_TILE = ROWS // GRP
ROW_BOUND, ROW_GOFF, ROW_EXPERT, TAB_ROWS = 32, 33, 34, 40
SLOT_GROUPS = 256


def cdiv(a, b):
    return (a + b - 1) // b


def spans(d):
    return [(LANES * j, min(LANES, d - LANES * j)) for j in range(cdiv(d, LANES))]


any_space = pl.BlockSpec(memory_space=pl.ANY)
in_vmem = pl.BlockSpec(memory_space=pltpu.VMEM)


def sorted_list(expert_ids, gate_vals):
    n_tok, top = expert_ids.shape
    n = n_tok * top
    keys = expert_ids.reshape(n) * n + jnp.arange(n, dtype=I32)
    keys, gates = lax.sort((keys, gate_vals.reshape(n)), num_keys=1)
    return ((keys % n) // top).astype(F32), gates


def plan_kernel(n_layers, n_local, n_tok, list_rows, all_ref, tab_ref, idx_ref, gate_ref):
    n_mine = n_local // 2
    core, ep = lax.axis_index('core'), lax.axis_index('ep')
    list_len = list_rows * LANES
    lane = lambda n: lax.broadcasted_iota(I32, (n, LANES), 1).astype(F32)
    sub = lambda n: lax.broadcasted_iota(I32, (n, LANES), 0).astype(F32)
    over_lanes = lambda v: jnp.sum(v, axis=1, keepdims=True)
    over_subs = lambda v: jnp.sum(v, axis=0, keepdims=True)
    l16, s16 = lane(n_mine), sub(n_mine)
    for l in range(n_layers):
        cnt = all_ref[:, 2 * n_layers * list_rows + l, :]
        ends = cnt
        step = 1
        while step < 2 * n_local:
            ends = ends + jnp.where(lane(8) >= step, pltpu.roll(ends, step, 1), 0.0)
            step *= 2
        starts = ends - cnt
        second = (ep > 0)
        local = lambda v: jnp.where(lane(8) < n_local, jnp.where(second, pltpu.roll(v, LANES - n_local, 1), v), 0.0)
        cnt, starts = local(cnt), local(starts)
        grp = jnp.floor((cnt + (GRP - 0.5)) * (1.0 / GRP))
        tiles = [jnp.maximum(1.0, jnp.floor((over_subs(grp[h * N_SRC:(h + 1) * N_SRC]) + (PER_TILE - 0.5)) * (1.0 / PER_TILE)))
                 for h in range(2)]
        load = jnp.where(lane(1) < n_local, 3.0 * tiles[0] + 2.0 * tiles[1], -1.0)
        wide = jnp.broadcast_to(load, (n_local, LANES))
        col = over_lanes(jnp.where(lane(n_local) == sub(n_local), wide, 0.0))
        ahead = (col > wide) | ((col == wide) & (sub(n_local) < lane(n_local)))
        rank = over_subs(jnp.where(ahead, 1.0, 0.0))
        odd = s16 - 2.0 * jnp.floor(s16 * 0.5 + 0.25)
        flip = jnp.where(core > 0, 1.0 - odd, odd)
        pick = (jnp.broadcast_to(rank, (n_mine, LANES)) == 2.0 * s16 + flip) & (l16 < n_local)
        mine = lambda row: over_lanes(jnp.where(pick, jnp.broadcast_to(row, (n_mine, LANES)), 0.0))
        as_row = lambda c: over_subs(jnp.where(l16 == s16, c, 0.0))
        experts = as_row(mine(lane(1)))
        for h in range(2):
            at = (h * n_layers + l) * TAB_ROWS
            off = jnp.zeros((n_mine, 1), F32)
            pos = [jnp.zeros((n_mine, LANES), F32) for _ in range(SLOT_GROUPS // LANES)]
            for s in range(N_SRC):
                r = h * N_SRC + s
                c, st = mine(cnt[r:r + 1]), mine(starts[r:r + 1]) + float(s * list_len)
                ng = jnp.floor((c + (GRP - 0.5)) * (1.0 / GRP))
                for i in range(len(pos)):
                    rel = l16 + float(LANES * i) - off
                    code = (st + GRP * rel) * 16.0 + jnp.minimum(float(GRP), c - GRP * rel)
                    pos[i] = jnp.where((rel >= 0) & (rel < ng), code, pos[i])
                off = off + ng
            for i in range(len(pos)):
                tab_ref[pl.ds(at + i, n_mine, stride=len(pos)), :] = pos[i].astype(I32)
            n_tiles = jnp.maximum(1.0, jnp.floor((off + (PER_TILE - 0.5)) * (1.0 / PER_TILE)))
            bounds = over_subs(jnp.where(s16 < l16, n_tiles, 0.0))
            before = over_lanes(jnp.where(l16 == s16, jnp.broadcast_to(bounds, (n_mine, LANES)), 0.0))
            t = jnp.minimum(l16, over_subs(jnp.broadcast_to(n_tiles, (n_mine, LANES))) - 1.0)
            inside = (t >= before) & (t < before + n_tiles)
            goff = over_subs(jnp.where(inside, s16 * float(SLOT_GROUPS) + (t - before) * float(PER_TILE), 0.0))
            rows = [(ROW_BOUND, bounds), (ROW_GOFF, goff), (ROW_EXPERT, experts)]
            for row, value in rows:
                tab_ref[at + row:at + row + 1, :] = value.astype(I32)
    for h in range(2):
        for l in range(n_layers):
            pad = (h * n_layers + l) * (N_SRC * list_rows + 8) + N_SRC * list_rows
            gate_ref[pad:pad + 8, :] = jnp.zeros((8, LANES), F32)
            for s in range(N_SRC):
                to = ((h * n_layers + l) * N_SRC + s) * list_rows
                toks = all_ref[h * N_SRC + s, l * list_rows:(l + 1) * list_rows, :]
                idx_ref[to:to + list_rows, :] = ((toks + float(s * n_tok)) * float(PITCH)).astype(I32)
                to = (h * n_layers + l) * (N_SRC * list_rows + 8) + s * list_rows
                gate_ref[to:to + list_rows, :] = all_ref[
                    h * N_SRC + s, (n_layers + l) * list_rows:(n_layers + l + 1) * list_rows, :]


def plan(shared, n_layers, n_local, n_tok, list_rows):
    n_tab = 2 * n_layers * TAB_ROWS
    n_list = 2 * n_layers * N_SRC * list_rows
    n_gate = 2 * n_layers * (N_SRC * list_rows + 8)
    tab, idx, gates = pl.pallas_call(
        functools.partial(plan_kernel, n_layers, n_local, n_tok, list_rows),
        out_shape=[jax.ShapeDtypeStruct((n_tab, LANES), I32), jax.ShapeDtypeStruct((n_list, LANES), I32),
                   jax.ShapeDtypeStruct((n_gate, LANES), F32)],
        in_specs=[in_vmem], out_specs=[in_vmem] * 3,
        cost_estimate=pl.CostEstimate(flops=10 ** 7, bytes_accessed=10 ** 6, transcendentals=0),
        name="plan",
    )(shared)
    return tab.reshape(-1), idx.reshape(-1), gates


def expert_kernel(cfg, *refs):
    fwd, bwd, own, n_blk, d, ff, at0, list_at, list_len, p_f32, n_alias = cfg
    refs = list(refs)
    take = lambda n: [refs.pop(0) for _ in range(n)]
    tab_ref, idx_hbm, gate_ref = take(3)
    u_refs = take(N_SRC)
    dy_refs = take(N_SRC) if bwd else []
    wg_ref, wu_ref, wd_ref = take(3)
    prev = take(1)[0] if bwd and not own else None
    take(n_alias)
    y_outs = take(N_SRC) if fwd else []
    du_outs = take(N_SRC) if bwd and own else []
    grad = take(1)[0] if bwd and own else None
    finals = take(3) if bwd and not own else None
    sent = take(1)[0] if bwd and not own else None
    table, gat = take(2)
    acc, row_ref = take(2) if own else (None, None)
    gu_ref, g_ref, x_u = take(3)
    x_c = take(1)[0] if bwd else None
    ab_ref = take(1)[0]
    dh_ref = take(1)[0] if bwd else None
    h_ref = take(1)[0]
    dab_ref = take(1)[0] if bwd else None
    sums = take(1)[0] if bwd and not own else None
    idx, list_sem = take(2)
    stage_f, stage_b, out_sem = take(3) if own else (None, None, None)

    step = pl.program_id(0)
    cols = spans(d)
    lo = ff // 256 * 256
    hi = ff - lo
    b_at, g_at = at0 + ROW_BOUND * LANES, at0 + ROW_GOFF * LANES
    dot = functools.partial(lax.dot_general, preferred_element_type=F32)
    nn = (((1,), (0,)), ((), ()))
    nt = (((1,), (1,)), ((), ()))
    tn = (((0,), (0,)), ((), ()))
    al = lambda v, m=PITCH: pl.multiple_of(v, m)
    tok_rows = PITCH * N_SRC * n_blk

    glane = lax.broadcasted_iota(I32, (GRP, LANES), 1)
    gsub = lax.broadcasted_iota(I32, (GRP, LANES), 0)

    def group(tile, q):
        return tab_ref[at0 + tab_ref[g_at + tile] + q]

    def gather(tile, q):
        ids = idx.at[pl.ds(group(tile, q) >> 4, GRP)]
        for k in range(GRP):
            gat[pl.ds(al((q * GRP + k) * PITCH), PITCH), :] = table[pl.ds(al(ids[k]), PITCH), :]

    def gate_column(code):
        pos = code >> 4
        row, shift = pos >> 7, pos & (LANES - 1)
        want = glane == gsub + shift
        over = glane == gsub + (shift - LANES)
        here = gate_ref[pl.ds(row, GRP, stride=0), :]
        there = gate_ref[pl.ds(row + 1, GRP, stride=0), :]
        v = jnp.where(want, here, jnp.where(over, there, 0.0))
        return jnp.where(gsub < (code & 15), jnp.sum(v, axis=1, keepdims=True), 0.0)

    def scatter(tile, q):
        ids = idx.at[pl.ds(group(tile, q) >> 4, GRP)]
        new = []
        for k in range(GRP):
            at = pl.ds(al(ids[k]), PITCH)
            new.append((at, acc[at, :] + row_ref[pl.ds(al((q * GRP + k) * PITCH), PITCH), :]))
        for at, value in reversed(new):
            acc[at, :] = value

    def convert(tile):
        for q in range(0, PER_TILE, 2):
            part = []
            for p in (q, q + 1):
                code = group(tile, p)
                rows = [gat[pl.ds(GRP * PITCH * p + j, GRP, stride=PITCH), :] for j in range(PITCH if bwd else HALF)]
                real = gsub < (code & 15)
                gate = gate_column(code)
                g_ref[GRP * p:GRP * (p + 1), :] = gate
                part.append([jnp.where(real, v, 0.0) for v in rows[:HALF]] + [v * gate for v in rows[HALF:]])
            at = slice(GRP * q, GRP * (q + 2))
            for x, o in ((x_u, 0), (x_c, HALF)):
                if x is None:
                    continue
                for j, (c, w) in enumerate(cols):
                    both = jnp.concatenate([part[0][o + j], part[1][o + j]], axis=0)
                    x[at, c:c + w] = both[:, :w].astype(BF16)

    @pl.when(step == 0)
    def _():
        src = pl.ds(list_at, N_SRC * list_len)
        lists = pltpu.make_async_copy(idx_hbm.at[src], idx.at[pl.ds(0, N_SRC * list_len)], list_sem)
        lists.start()
        if own:
            def clear(c, _):
                for k in range(4):
                    acc[pl.ds(al(c * 2048 + 512 * k, 512), 512), :] = jnp.zeros((512, LANES), F32)
                return 0

            lax.fori_loop(0, tok_rows // 2048, clear, 0)
            row_ref[...] = jnp.zeros(row_ref.shape, F32)
        rows = 256
        for srcs, o, seed in ((u_refs, 0, fwd), (dy_refs, HALF, own)):
            for s, ref in enumerate(srcs):
                def fill(c, _, ref=ref, o=o, seed=seed, s=s):
                    r = al(c * rows, rows)
                    at = PITCH * (s * n_blk + r) + o
                    for j in range(HALF):
                        vals = ref[0, pl.ds(r, rows), LANES * j:LANES * (j + 1)].astype(F32)
                        to = pl.ds(at + j, rows, stride=PITCH)
                        table[to, :] = vals
                        if seed and s == 0:
                            acc[to, :] = vals
                    return 0

                lax.fori_loop(0, n_blk // rows, fill, 0)
        lists.wait()
        for k in range(GRP):
            idx[N_SRC * list_len + k] = 0

        def first(q, _):
            gather(0, 2 * q)
            gather(0, 2 * q + 1)
            return 0

        lax.fori_loop(0, PER_TILE // 2, first, 0)
        convert(0)

    for i, w in enumerate((wg_ref, wu_ref)):
        gu_ref[i * lo:(i + 1) * lo, :] = w[0, 0, 0:lo, :]
        gu_ref[2 * lo + i * hi:2 * lo + (i + 1) * hi, :] = w[0, 0, lo:, :]
    total = grad if own else sums
    if bwd:
        total[...] = jnp.zeros(total.shape, F32) if own else prev[0]

    def put_rows(o, value, s0=0):
        value = value.astype(BF16).astype(F32)
        n = value.shape[0]
        for j, (c, w) in enumerate(cols):
            row_ref[pl.ds(PITCH * s0 + o + j, n, stride=PITCH), 0:w] = value[:, c:c + w] * g_ref[s0:s0 + n, 0:w]

    low = lax.broadcasted_iota(I32, (16, 2 * hi), 1) < hi

    def middle(a, b, dh):
        sig = 0.5 * jnp.tanh(0.5 * a) + 0.5
        act = a * sig
        h = act * b
        if dh is None:
            return h, None, None
        slope = sig * (1.0 + a * (1.0 - sig))
        return h, dh * b * slope, dh * act

    def tile(t, _):
        for q in range(PER_TILE):
            if own:
                scatter(jnp.maximum(t - 1, 0), q)
            gather(t + 1, q)
        part = ROWS // 2
        for s0 in range(0, ROWS, part):
            sl = slice(s0, s0 + part)
            ab_ref[sl, :] = dot(x_u[sl, :], gu_ref[...], nt)
            if bwd:
                dh_ref[sl, :] = dot(x_c[sl, :], wd_ref[0, 0], nt)
        for r in range(0, ROWS, 16):
            rows = slice(r, r + 16)
            for c in range(0, lo, LANES):
                h, da, db = middle(ab_ref[rows, c:c + LANES], ab_ref[rows, lo + c:lo + c + LANES],
                                   dh_ref[rows, c:c + LANES] if bwd else None)
                h_ref[rows, c:c + LANES] = h.astype(BF16)
                if bwd:
                    dab_ref[rows, c:c + LANES] = da.astype(BF16)
                    dab_ref[rows, lo + c:lo + c + LANES] = db.astype(BF16)
            a = ab_ref[rows, 2 * lo:]
            b = pltpu.roll(a, hi, 1)
            dh = dh_ref[rows, lo:] if bwd else None
            if bwd:
                dh = jnp.concatenate([dh, dh], axis=1)
            h, da, db = middle(a, b, dh)
            h_ref[rows, lo:] = h[:, :hi].astype(BF16)
            if bwd:
                dab_ref[rows, 2 * lo:] = jnp.where(low, da, pltpu.roll(db, hi, 1)).astype(BF16)
        for s0 in range(0, ROWS, part):
            sl = slice(s0, s0 + part)
            if fwd:
                put_rows(0, dot(h_ref[sl, :], wd_ref[0, 0], nn), s0)
            if bwd and own:
                put_rows(HALF, dot(dab_ref[sl, :], gu_ref[...], nn), s0)
        if bwd:
            view = total.at[0] if own else total
            view[0:2 * ff, :] += dot(dab_ref[...], x_u[...], tn)
            view[2 * ff:, :] += dot(h_ref[...], x_c[...], tn)
        convert(t + 1)
        return 0

    lax.fori_loop(tab_ref[b_at + step], tab_ref[b_at + step + 1], tile, 0)
    if bwd and not own:
        for out in ([f.at[0, 0] for f in finals], [sent.at[0, i] for i in range(3)]):
            for i in range(2):
                out[i][0:lo, :] = sums[i * lo:(i + 1) * lo, :].astype(BF16)
                out[i][lo:, :] = sums[2 * lo + i * hi:2 * lo + (i + 1) * hi, :].astype(BF16)
            out[2][...] = sums[2 * ff:, :].astype(BF16)

    if own:
        @pl.when(step == pl.num_programs(0) - 1)
        def _():
            end = tab_ref[b_at + step + 1] - 1
            lax.fori_loop(0, PER_TILE, lambda q, _: (scatter(end, q), 0)[1], 0)
            chunk = stage_f.shape[1]
            flights = {}
            n = 0
            for o, out in ((HALF, du_outs), (0, y_outs)):
                for s in range(N_SRC if out else 0):
                    wide = s == 0 or p_f32
                    stage = stage_f if wide else stage_b
                    for c in range(n_blk // chunk):
                        key = (wide, n % 2)
                        if key in flights:
                            flights.pop(key).wait()
                        for j in range(HALF):
                            rows = pl.ds(PITCH * (s * n_blk + c * chunk) + o + j, chunk, stride=PITCH)
                            stage[n % 2, :, LANES * j:LANES * (j + 1)] = acc[rows, :].astype(stage.dtype)
                        flights[key] = pltpu.make_async_copy(
                            stage.at[n % 2], out[s].at[pl.ds(c * chunk, chunk), :], out_sem.at[2 * wide + n % 2])
                        flights[key].start()
                        n += 1
            for copy in flights.values():
                copy.wait()


def run_experts(routes, layer, half, u, dy, weights, prev, finals, fwd, own, p_f32=False):
    tab, idx, gates = routes
    bwd = dy is not None
    wg, wu, wd = weights
    _, n_blk, wide = u[0].shape
    n_layers, n_local, ff, d = wd.shape
    n_exp = n_local // 2
    row_id = half * n_layers + layer
    at0 = row_id * TAB_ROWS * LANES
    e_at = at0 + ROW_EXPERT * LANES
    list_len = idx.shape[0] // (2 * n_layers * N_SRC)

    block = lambda i: pl.BlockSpec((1, n_blk, wide), lambda e, *_: (i, 0, 0), pipeline_mode=pl.Buffered(1))
    blocks = [block(0), block(1)] * 2
    weight = pl.BlockSpec((1, 1, ff, d), lambda e, tab: (layer, tab[e_at + e], 0, 0))
    partial = pl.BlockSpec((1, 3 * ff, d), lambda e, *_: (e, 0, 0))

    four = lambda pairs: [pairs[0], pairs[0], pairs[1], pairs[1]]
    operands = [idx, gates] + four(u) + (four(dy) if bwd else []) + [wg, wu, wd]
    gate_rows = N_SRC * list_len // LANES + 8
    gate_spec = pl.BlockSpec((gate_rows, LANES), lambda e, *_: (row_id, 0), pipeline_mode=pl.Buffered(1))
    in_specs = [any_space, gate_spec] + blocks * (1 + bwd) + [weight] * 3
    out_shape, out_specs, aliases = [], [], {}
    for use in (fwd, bwd and own):
        if use:
            out_shape += [jax.ShapeDtypeStruct((n_blk, wide), F32 if s == 0 or p_f32 else BF16) for s in range(N_SRC)]
            out_specs += [any_space] * N_SRC
    if bwd and own:
        out_shape.append(jax.ShapeDtypeStruct((n_exp, 3 * ff, d), F32))
        out_specs.append(partial)
    if bwd and not own:
        operands.append(prev)
        in_specs.append(partial)
        for i, f in enumerate(finals or ()):
            aliases[1 + len(operands)] = i
            operands.append(f)
            in_specs.append(any_space)
        out_shape += [jax.ShapeDtypeStruct((n_layers, n_local, ff, d), BF16)] * 3
        out_specs += [weight] * 3
        out_shape.append(jax.ShapeDtypeStruct((n_exp, 3, ff, d), BF16))
        out_specs.append(pl.BlockSpec((1, 3, ff, d), lambda e, *_: (e, 0, 0, 0)))
    table = pltpu.VMEM((PITCH * N_SRC * n_blk, LANES), F32)
    rows = pltpu.VMEM((PITCH * ROWS, LANES), F32)
    mid = lambda n, dt: pltpu.VMEM((ROWS, n), dt)
    scratch = [table, rows] * (1 + own)
    scratch += [pltpu.VMEM((2 * ff, d), BF16), mid(LANES, F32)] + [mid(d, BF16)] * (1 + bwd) + [mid(2 * ff, F32)]
    scratch += [mid(ff, F32)] * bwd + [mid(ff, BF16)] + [mid(2 * ff, BF16)] * bwd
    if bwd and not own:
        scratch.append(pltpu.VMEM((3 * ff, d), F32))
    scratch += [pltpu.SMEM((N_SRC * list_len + 128,), I32), pltpu.SemaphoreType.DMA]
    if own:
        scratch += [pltpu.VMEM((2, 256, wide), F32), pltpu.VMEM((2, 256, wide), BF16), pltpu.SemaphoreType.DMA((4,))]
    passes = 2 + fwd + bwd * (4 + 2 * own)
    flops = 2 * d * ff * passes * n_blk * N_SRC * 2
    cfg = (fwd, bwd, own, n_blk, d, ff, at0, row_id * N_SRC * list_len, list_len, p_f32, len(aliases))
    return pl.pallas_call(
        functools.partial(expert_kernel, cfg),
        out_shape=out_shape,
        grid_spec=pltpu.PrefetchScalarGridSpec(
            num_scalar_prefetch=1, grid=(n_exp,), in_specs=in_specs, out_specs=out_specs, scratch_shapes=scratch),
        input_output_aliases=aliases,
        compiler_params=pltpu.CompilerParams(dimension_semantics=("arbitrary",), vmem_limit_bytes=VMEM_LIMIT),
        cost_estimate=pl.CostEstimate(flops=flops, bytes_accessed=3 * 2 * n_exp * d * ff, transcendentals=0),
        name=f"experts_{'f' if fwd else ''}{'b' if bwd else ''}_{'own' if own else 'other'}_{layer}",
    )(tab, *operands)


def place_kernel(layer, n_exp, tab_at, tab_ref, got_ref, *refs):
    outs, (buf, in_sem, out_sem) = refs[3:6], refs[6:]
    reads = [pltpu.make_async_copy(got_ref.at[i], buf.at[i], in_sem.at[i]) for i in range(n_exp)]
    for read in reads:
        read.start()
    writes = []
    for i, read in enumerate(reads):
        read.wait()
        e = tab_ref[tab_at + i]
        for k, out in enumerate(outs):
            writes.append(pltpu.make_async_copy(buf.at[i, k], out.at[layer, e], out_sem.at[i, k]))
            writes[-1].start()
    for write in writes:
        write.wait()


def place(partner, layer, got, finals):
    n_exp = got.shape[0]
    return pl.pallas_call(
        functools.partial(place_kernel, layer, n_exp, layer * n_exp),
        out_shape=[jax.ShapeDtypeStruct(f.shape, f.dtype) for f in finals],
        grid_spec=pltpu.PrefetchScalarGridSpec(
            num_scalar_prefetch=1, grid=(1,), in_specs=[any_space] * 4, out_specs=[any_space] * 3,
            scratch_shapes=[pltpu.VMEM(got.shape, got.dtype), pltpu.SemaphoreType.DMA((n_exp,)),
                            pltpu.SemaphoreType.DMA((n_exp, 3))]),
        input_output_aliases={2: 0, 3: 1, 4: 2},
        compiler_params=pltpu.CompilerParams(vmem_limit_bytes=VMEM_LIMIT),
        cost_estimate=pl.CostEstimate(flops=0, bytes_accessed=4 * got.size, transcendentals=0),
        name=f"place_{layer}",
    )(partner, got, *finals)


def peer(rel):
    return {name: (lax.axis_index(name) + ((rel >> bit) & 1)) % 2 for bit, name in enumerate(("ep", "core", "x"))}


def meet(rels):
    barrier = pltpu.get_barrier_semaphore()
    for rel in rels:
        pl.semaphore_signal(barrier, inc=1, device_id=peer(rel), device_id_type=MESH)
    pl.semaphore_wait(barrier, len(rels))


def remote(src, dst, send, recv, rel):
    return pltpu.make_async_remote_copy(src_ref=src, dst_ref=dst, send_sem=send, recv_sem=recv,
                                        device_id=peer(rel), device_id_type=MESH)


def share_kernel(n_rel, mine_ref, all_ref, send_sem, recv_sem):
    meet(range(1, n_rel))
    copies = [remote(mine_ref, all_ref.at[rel], send_sem.at[rel], recv_sem.at[rel], rel) for rel in range(1, n_rel)]
    for copy in copies:
        copy.start()
    all_ref[0] = mine_ref[...]
    for copy in copies:
        copy.wait()


def share(mine, n_rel):
    return pl.pallas_call(
        functools.partial(share_kernel, n_rel),
        out_shape=jax.ShapeDtypeStruct((n_rel,) + mine.shape, mine.dtype),
        in_specs=[in_vmem],
        out_specs=in_vmem,
        scratch_shapes=[pltpu.SemaphoreType.DMA((n_rel,)), pltpu.SemaphoreType.DMA((n_rel,))],
        compiler_params=pltpu.CompilerParams(collective_id=0, has_side_effects=True),
        cost_estimate=pl.CostEstimate(flops=10 ** 7, bytes_accessed=mine.size * 4 * n_rel, transcendentals=0),
        name="share_lists",
    )(mine)


def blocks_kernel(cfg, *refs):
    n_chunk, reduce, across, back, d = cfg
    refs = list(refs)
    take = lambda n: [refs.pop(0) for _ in range(n)]
    parts = take(N_SRC)
    m_ref, o_total, o_a, o_b = take(4)
    o_xa, o_xb = take(2) if across else (None, None)
    in_f, in_b, got_f, s_buf, r_buf, t_buf, u_buf, load, send, recv, put = take(11)
    n_rows = t_buf.shape[0] // n_chunk
    cut = [pl.ds(k * n_rows, n_rows) for k in range(n_chunk)]
    chunks = range(n_chunk)
    loads = {}
    for i, part in enumerate(parts[:2] if reduce else parts):
        buf = in_f.at[i] if reduce or i == 0 else in_b.at[i - 1]
        for k in chunks:
            loads[i, k] = pltpu.make_async_copy(part.at[cut[k]], buf.at[cut[k]], load.at[i, k])
    order = (1, 0) if reduce else range(N_SRC)
    for i in order:
        for k in chunks:
            loads[i, k].start()
    u_buf[...] = jnp.zeros(u_buf.shape, BF16)
    meet((Y, CORE, X) if across else (Y, CORE))
    links = []

    def link(src, dst, rel):
        n = len(links)
        links.append([remote(src.at[cut[k]], dst.at[cut[k]], send.at[n, k], recv.at[n, k], rel) for k in chunks])
        return links[-1]

    if reduce:
        first = link(parts[3], got_f.at[1], CORE)
        second = link(parts[2], got_f.at[0], CORE)
        over = link(s_buf, r_buf, Y)
        for copies in (first, second):
            for copy in copies:
                copy.start()
        for k in chunks:
            loads[1, k].wait()
            first[k].wait_recv()
            s_buf[cut[k], :] = (in_f[1, cut[k], :] + got_f[1, cut[k], :]).astype(BF16)
            over[k].start()
    to_y = link(u_buf, o_a.at[1], Y)
    to_core = link(u_buf, o_b.at[0], CORE)
    to_x = link(u_buf, o_xa.at[0], X) if across else None
    puts = []
    for k in chunks:
        if reduce:
            loads[0, k].wait()
            second[k].wait_recv()
            over[k].wait_recv()
            total = in_f[0, cut[k], :] + got_f[0, cut[k], :] + r_buf[cut[k], :].astype(F32)
        else:
            for i in range(N_SRC):
                loads[i, k].wait()
            total = in_f[0, cut[k], :]
            for i in range(N_SRC - 1):
                total = total + in_b[i, cut[k], :].astype(F32)
        total = total.astype(BF16)
        t_buf[cut[k], :] = total
        dims = (((1,), (1 if back else 0,)), ((), ()))
        mixed = lax.dot_general(total[:, :d], m_ref[...], dims, preferred_element_type=F32)
        u_buf[cut[k], 0:d] = (total[:, :d].astype(F32) + mixed).astype(BF16)
        to_y[k].start()
        to_core[k].start()
        if across:
            to_x[k].start()
        puts.append(pltpu.make_async_copy(u_buf.at[cut[k]], o_a.at[0, cut[k]], put.at[0, k]))
        puts.append(pltpu.make_async_copy(t_buf.at[cut[k]], o_total.at[cut[k]], put.at[1, k]))
        for copy in puts[-2:]:
            copy.start()
    on = link(o_a.at[1], o_b.at[1], CORE)
    on_x = link(o_a.at[1], o_xa.at[1], X) if across else None
    for k in chunks:
        to_y[k].wait_recv()
        on[k].start()
        if across:
            on_x[k].start()
    if across:
        last = [link(o_xa.at[i], o_xb.at[i], CORE) for i in range(2)]
        for i, arrived in enumerate((to_x, on_x)):
            for k in chunks:
                arrived[k].wait_recv()
                last[i][k].start()
    waited = [to_y] + ([first, second, over] if reduce else []) + ([to_x, on_x] if across else [])
    for copies in links:
        for copy in copies:
            if any(copies is w for w in waited):
                copy.wait_send()
            else:
                copy.wait()
    for copy in puts:
        copy.wait()


def complete_blocks(parts, m, reduce, across, back, ident, n_chunk=4):
    n_blk, wide = parts[0].shape
    d = m.shape[0]
    sem = lambda *s: pltpu.SemaphoreType.DMA(s)
    pair = jax.ShapeDtypeStruct((2, n_blk, wide), BF16)
    buf = lambda n, dt: pltpu.VMEM((n, n_blk, wide) if n else (n_blk, wide), dt)
    return pl.pallas_call(
        functools.partial(blocks_kernel, (n_chunk, reduce, across, back, d)),
        out_shape=[jax.ShapeDtypeStruct((n_blk, wide), BF16)] + [pair] * (4 if across else 2),
        in_specs=[any_space] * N_SRC + [in_vmem],
        out_specs=[any_space] * (5 if across else 3),
        scratch_shapes=[buf(2, F32), buf(3, BF16), buf(2, F32), buf(0, BF16), buf(0, BF16), buf(0, BF16), buf(0, BF16),
                        sem(4, n_chunk), sem(10, n_chunk), sem(10, n_chunk), sem(2, n_chunk)],
        compiler_params=pltpu.CompilerParams(collective_id=ident, has_side_effects=True, vmem_limit_bytes=VMEM_LIMIT),
        cost_estimate=pl.CostEstimate(flops=10 ** 8, bytes_accessed=n_blk * wide * 40, transcendentals=0),
        name=f"complete_blocks_{ident}",
    )(*parts, m)


def total_kernel(n_chunk, g_ref, o_ref, give, got, s_buf, y_buf, t_buf, x_buf, z_buf, send, recv):
    core = lax.axis_index('core')
    n_rows = o_ref.shape[1] // n_chunk
    cut = [pl.ds(k * n_rows, n_rows) for k in range(n_chunk)]
    first = core > 0
    give[...] = jnp.where(first, g_ref[0], g_ref[1])
    meet((Y, CORE, X))
    copies = [[remote(src.at[cut[k]], dst.at[cut[k]], send.at[i, k], recv.at[i, k], rel) for k in range(n_chunk)]
              for i, (src, dst, rel) in enumerate(((give, got, CORE), (s_buf, y_buf, Y), (t_buf, x_buf, X)))]
    for copy in copies[0]:
        copy.start()
    for k in range(n_chunk):
        copies[0][k].wait_recv()
        mine = jnp.where(first, g_ref[1, cut[k], :], g_ref[0, cut[k], :])
        s_buf[cut[k], :] = (mine + got[cut[k], :]).astype(BF16)
        copies[1][k].start()
    for k in range(n_chunk):
        copies[1][k].wait_recv()
        t_buf[cut[k], :] = (s_buf[cut[k], :].astype(F32) + y_buf[cut[k], :].astype(F32)).astype(BF16)
        copies[2][k].start()
    for k in range(n_chunk):
        copies[2][k].wait_recv()
        got[cut[k], :] = t_buf[cut[k], :].astype(F32) + x_buf[cut[k], :].astype(F32)
    for group in copies:
        for copy in group:
            copy.wait_send()
    s_buf[...] = got[...].astype(BF16)
    swap = remote(s_buf, z_buf, send.at[3, 0], recv.at[3, 0], CORE)
    swap.start()
    swap.wait()
    o_ref[0] = jnp.where(first, z_buf[...], s_buf[...])
    o_ref[1] = jnp.where(first, s_buf[...], z_buf[...])


def total_grads(g, ident, n_chunk=4):
    _, d, _ = g.shape
    buf = lambda dt: pltpu.VMEM((d, d), dt)
    return pl.pallas_call(
        functools.partial(total_kernel, n_chunk),
        out_shape=jax.ShapeDtypeStruct(g.shape, BF16),
        in_specs=[in_vmem], out_specs=in_vmem,
        scratch_shapes=[buf(F32), buf(F32), buf(BF16), buf(BF16), buf(BF16), buf(BF16), buf(BF16),
                        pltpu.SemaphoreType.DMA((4, n_chunk)), pltpu.SemaphoreType.DMA((4, n_chunk))],
        compiler_params=pltpu.CompilerParams(collective_id=ident, has_side_effects=True),
        cost_estimate=pl.CostEstimate(flops=10 ** 7, bytes_accessed=g.size * 8, transcendentals=0),
        name="total_grads",
    )(g)


def solution(mesh):
    ep_size, dp_size = mesh.shape['ep'], mesh.shape['dp']
    sub = Mesh(mesh.devices.reshape(ep_size, dp_size // 2, 2), ('ep', 'x', 'core'))
    tok_axes = ('x', 'core', 'ep')
    tok_spec = P(tok_axes, None)
    route_spec = P(None, tok_axes, None)
    whole_spec = P(None, None, None)
    expert_spec = P(None, 'ep', None, None)
    flip = [(0, 1), (1, 0)]
    move = lambda v, axis: lax.ppermute(v, axis, flip)
    move_diag = lambda v: lax.ppermute(v, ('ep', 'core'), [(0, 3), (1, 2), (2, 1), (3, 0)])
    fence = lax.optimization_barrier

    def device_step(tokens, d_out, expert_ids, gate_vals, w_mix, w_gate, w_up, w_down):
        n_layers, d = w_mix.shape[0], w_mix.shape[1]
        n_tok = tokens.shape[0]
        top = expert_ids.shape[2]
        n_local = w_gate.shape[1]
        n_exp = n_local * ep_size
        n = n_tok * top
        n_rel = 2 * N_SRC
        wide = cdiv(d, LANES) * LANES
        weights = (jnp.swapaxes(w_gate, 2, 3), jnp.swapaxes(w_up, 2, 3), w_down)
        pad = lambda v: jnp.pad(v, ((0, 0), (0, wide - d)))
        send_three = lambda p: [move(p[1], 'ep'), move(p[2], 'core'), move_diag(p[3])]

        def own_sum(p, got):
            return sum([g.astype(F32) for g in got], p)[:, :d].astype(BF16)

        u0 = pad((tokens.astype(F32) + jnp.dot(tokens, w_mix[0], preferred_element_type=F32)).astype(BF16))
        u0_far = move(u0, 'ep')
        lists = [sorted_list(expert_ids[l], gate_vals[l]) for l in range(n_layers)]
        counts = jnp.sum((expert_ids.reshape(n_layers, n, 1) == jnp.arange(n_exp, dtype=I32)).astype(F32), axis=1)
        packed = jnp.concatenate([jnp.concatenate([v[0] for v in lists] + [v[1] for v in lists]).reshape(-1, LANES),
                                  jnp.pad(counts, ((0, 8 - n_layers), (0, LANES - n_exp)))], axis=0)
        shared = share(packed, n_rel)
        routes = plan(shared, n_layers, n_local, n_tok, n // LANES)
        row = lambda l: lax.slice_in_dim(routes[0], (l * TAB_ROWS + ROW_EXPERT) * LANES,
                                         (l * TAB_ROWS + ROW_EXPERT) * LANES + n_local // 2)
        partner = move(jnp.concatenate([row(l) for l in range(n_layers)]), 'core')
        u0_a = jnp.stack([u0, u0_far])
        u0_b = move(u0_a, 'core')

        dy, shared = fence((pad(d_out), shared))
        dy_a = jnp.stack([dy, move(dy, 'ep')])
        part = run_experts(routes, 0, 0, (u0_a, u0_b), None, weights, None, None, True, True, p_f32=True)
        dy_b = move(dy_a, 'core')
        y0, u1_a, u1_b, u1_xa, u1_xb = complete_blocks(part, w_mix[1], True, True, False, 1)
        dy_a, u0_a2, y0 = fence((dy_a, u0_a, y0))
        dy_xa, u0_xa = move(dy_a, 'x'), move(u0_a2, 'x')
        out = run_experts(routes, 1, 0, (u1_a, u1_b), (dy_a, dy_b), weights, None, None, True, True)
        y_part, du_part, g1 = out[:4], out[4:8], out[8]
        dy_xb, u0_xb = move(dy_xa, 'core'), move(u0_xa, 'core')
        got = send_three(du_part)
        out = run_experts(routes, 1, 1, (u1_xa, u1_xb), (dy_xa, dy_xb), weights, g1, None, False, False)
        got, out = fence((got, out))
        *finals, sent1 = out
        du1, dx_a, dx_b = complete_blocks([du_part[0], *got], w_mix[1], False, False, True, 2)
        dx_a, y_part, sent1 = fence((dx_a, y_part, sent1))
        dx_xa = move(dx_a, 'x')
        got_y = send_three(y_part)
        got1 = move(sent1, 'core')
        out = run_experts(routes, 0, 0, (u0_a, u0_b), (dx_a, dx_b), weights, None, None, False, True)
        dx_xa, got_y, out = fence((dx_xa, got_y, out))
        du_part, g0 = out[:4], out[4]
        dx_xb = move(dx_xa, 'core')
        got = send_three(du_part)
        out = run_experts(routes, 0, 1, (u0_xa, u0_xb), (dx_xa, dx_xb), weights, g0, finals, False, False)
        got, got1, out = fence((got, got1, out))
        *finals, sent0 = out
        got0 = move(sent0, 'core')
        du0 = own_sum(du_part[0], got)
        finals = place(partner, 1, got1, finals)
        y1 = own_sum(y_part[0], got_y)
        tx = lambda x, du: jnp.einsum('td,te->de', x, du, preferred_element_type=F32)
        g_mix = total_grads(jnp.stack([tx(tokens, du0), tx(y0[:, :d], du1[:, :d])]), 3)
        dx0 = (du0.astype(F32) + jnp.einsum('te,de->td', du0, w_mix[0], preferred_element_type=F32)).astype(BF16)
        finals, got0, g_mix = fence((finals, got0, g_mix))
        finals = place(partner, 0, got0, finals)
        return (y1, dx0, g_mix, jnp.swapaxes(finals[0], 2, 3), jnp.swapaxes(finals[1], 2, 3), finals[2])

    return jax.shard_map(device_step, mesh=sub,
                         in_specs=(tok_spec, tok_spec, route_spec, route_spec, whole_spec,
                                   expert_spec, expert_spec, expert_spec),
                         out_specs=(tok_spec, tok_spec, whole_spec, expert_spec, expert_spec, expert_spec),
                         check_vma=False)
```

time: 958 us -> 752 us (0.78)
  local copies, waits for them, and re-layouts: 171 us -> 18 us
  Pallas kernels: 577 us -> 554 us
  between operations: 15.1 us -> 1.41 us
  starting transfers between devices: 24.7 us -> 11.7 us
  other arithmetic: 36.9 us -> 25.1 us
    ppermute x28 -> x19, waiting for transfers between devices: 22.4 us -> 133 us  [solution(): move = lambda v, axis: lax.ppermute(v, axis, flip)]
    ppermute x9 -> x3, waiting for transfers between devices: 73.1 us -> 0.01 us  [solution(): lax.ppermute(v, ('ep', 'core'), [(0, 3), (1, 2), (2, 1), (3, 0)])]
    ppermute x34 -> x0, local copies, waits for them, and re-layouts: 70.7 us -> none  [the longest x25 54.3 us: solution(): move = lambda v, axis: lax.ppermute(v, axis, flip)]
    pallas_call x5, Pallas kernels: 465 us -> 396 us  [run_experts(): pl.pallas_call(functools.partial(expert_kernel, cfg), out_shape=out_shape...]
    pallas_call x3 -> x6, Pallas kernels: 84.9 us -> 141 us  [the longest x2 90.4 us: complete_blocks(): pl.pallas_call(functools.partial(blocks_kernel, (n_chunk, reduce, across,...]
    psum x1 -> x0, waiting for transfers between devices: 30.5 us -> none  [device_step(): g_mix0 = lax.psum(tx(tokens, du0).astype(BF16), tok_axes)]
    unnamed x81 -> x43, local copies, waits for them, and re-layouts: 32.7 us -> 9.35 us
    pallas_call x11 -> x0, local copies, waits for them, and re-layouts: 22.9 us -> none  [the longest x9 20.4 us: run_experts(): pl.pallas_call(functools.partial(expert_kernel, cfg), out_shape=out_shape...]
  transfers between devices with their start and end apart: 38 -> 22, of which waited for: 9 -> 7; matrix products, arithmetic and copies ran while one was open for 22% -> 5% of each run, Pallas kernels for 58% -> 52%
where the time goes in v3:
time: 752 us; the launch traced here: 750 us
  Pallas kernels  554 us (74%)
  waiting for transfers between devices  133 us (18%)
  other arithmetic  25.1 us (3%)
  local copies, waits for them, and re-layouts  18 us (2%)
  starting transfers between devices  11.7 us (2%)
    pallas_call x5, Pallas kernels, run_experts(): pl.pallas_call(functools.partial(expert_kernel, cfg), out_shape=out_shape...  396 us
    ppermute x19, waiting for transfers between devices, solution(): move = lambda v, axis: lax.ppermute(v, axis, flip)  133 us
    pallas_call x2, Pallas kernels, complete_blocks(): pl.pallas_call(functools.partial(blocks_kernel, (n_chunk, reduce, across,...  90.4 us
    pallas_call x2, Pallas kernels, place(): pl.pallas_call(functools.partial(place_kernel, layer, n_exp, layer * n_ex...  24.7 us
    pallas_call x1, Pallas kernels, total_grads(): pl.pallas_call(functools.partial(total_kernel, n_chunk), out_shape=jax.Sh...  22.4 us
    pallas_call x1, Pallas kernels, share(): pl.pallas_call(functools.partial(share_kernel, n_rel), out_shape=jax.Shap...  17.3 us
  transfers between devices with their start and end apart: 22, of which 7 were waited for; matrix products, arithmetic and copies ran while one was open for 5% of the time, Pallas kernels for 52%

profile of v3, /device:TPU:0, one launch (start us, length us, event | category | flops | bytes accessed | tf_op | source)
XLA Modules:
  0.0 750.1 jit_solution(17078711488827934946)
XLA Ops:
  5.1 3.4 collective-permute-start
  14.2 6.9 sort.47
  21.1 6.9 sort.46
  28.0 3.7 collective-permute-done
  34.6 17.3 %share_lists.1.all_ref = f32[8,264,128]{2,1,0:T(8,128)} custom-call(f32[264,128]{1,0:T(8,128)} %copy-done.15), custom_call_target="tpu_custom_call" | custom-call | flops 10000000 | bytes 1081344 | tf_op jit(solution)/shard_map/share_lists/pallas_call | solution.py:486
  53.5 3.1 plan.1
  58.4 19.3 %collective-permute-done.2 = bf16[1024,512]{1,0:T(8,128)(2,1)} collective-permute-done((bf16[1024,512]{1,0:T(8,128)(2,1)}, bf16[1024,512]{1,0:T(8,128)(2,1)}, u32[]{:S(2)}, u32[]{:S(2)}) %collective-permute-start.2) | collective-permute-done | bytes 1048608 | tf_op jit(solution)/shard_map/ppermute | solution.py:669
  77.7 2.8 pad_maximum_fusion.1.refs_7_.refs_8_
  80.4 61.5 %experts_f_own_0.1 = (f32[1024,512]{1,0:T(8,128)}, f32[1024,512]{1,0:T(8,128)}, f32[1024,512]{1,0:T(8,128)}, f32[1024,512]{1,0:T(8,128)}) custom-call(s32[20480]{0:T(1024)} %bitcast.58, s32[131072]{0:T(1024)} %bitcast.52, f32[1056,128]{1,0:T(8,128)} %get-tuple-element.102.refs_2_, bf16[2,1024,512]{2,1,0:T(8,128)(2,1)} %copy-done, ...), custom_call_target="tpu_custom_call" | custom-call | flops 7046430720 | bytes 13762560 | tf_op jit(solution)/shard_map/experts_f_own_0/pallas_call | solution.py:415
  142.0 59.3 %complete_blocks_1.1 = (bf16[1024,512]{1,0:T(8,128)(2,1)}, bf16[2,1024,512]{2,1,0:T(8,128)(2,1)}, bf16[2,1024,512]{2,1,0:T(8,128)(2,1)}, bf16[2,1024,512]{2,1,0:T(8,128)(2,1)}, bf16[2,1024,512]{2,1,0:T(8,128)(2,1)}) custom-call(f32[1024,512]{1,0:T(8,128)} %get-tuple-element.103.refs_0_, f32[1024,512]{1,0:T(8,128)} %get-tuple-element.104.refs_1_, ...), custom_call_target="tpu_custom_call" | custom-call | flops 100000000 | bytes 20971520 | tf_op jit(solution)/shard_map/complete_blocks_1/pallas_call | solution.py:598
  201.7 47.5 %collective-permute-done.7.refs_7_.refs_8_ = bf16[2,1024,512]{2,1,0:T(8,128)(2,1)} collective-permute-done((bf16[2,1024,512]{2,1,0:T(8,128)(2,1)}, bf16[2,1024,512]{2,1,0:T(8,128)(2,1)}, u32[]{:S(2)}, u32[]{:S(2)}) %collective-permute-start.7) | collective-permute-done | bytes 2097184 | tf_op jit(solution)/shard_map/ppermute | solution.py:669
  249.2 95.1 %experts_fb_own_1.1 = (f32[1024,512]{1,0:T(8,128)}, bf16[1024,512]{1,0:T(8,128)(2,1)}, bf16[1024,512]{1,0:T(8,128)(2,1)}, bf16[1024,512]{1,0:T(8,128)(2,1)}, f32...) custom-call(s32[20480]{0:T(1024)} %bitcast.59, ...), custom_call_target="tpu_custom_call" | custom-call | flops 21139292160 | bytes 13762560 | tf_op jit(solution)/shard_map/experts_fb_own_1/pallas_call | solution.py:415
  347.0 69.8 %experts_b_other_1.1 = (bf16[2,32,320,448]{3,2,1,0:T(8,128)(2,1)}, bf16[2,32,320,448]{3,2,1,0:T(8,128)(2,1)}, bf16[2,32,320,448]{3,2,1,0:T(8,128)(2,1)}, bf16[16,3,320,448]{3,2,1,0:T(8,128)(2,1)}) custom-call(s32[20480]{0:T(1024)} %bitcast.60, s32[131072]{0:T(1024)} %bitcast.54, f32[1056,128]{1,0:T(8,128)} %get-tuple-element.102.refs_2_, ...), custom_call_target="tpu_custom_call" | custom-call | flops 14092861440 | bytes 13762560 | tf_op jit(solution)/shard_map/experts_b_other_1/pallas_call | solution.py:415
  417.8 31.1 %complete_blocks_2.1 = (bf16[1024,512]{1,0:T(8,128)(2,1)}, bf16[2,1024,512]{2,1,0:T(8,128)(2,1)}, bf16[2,1024,512]{2,1,0:T(8,128)(2,1)}) custom-call(f32[1024,512]{1,0:T(8,128)} %get-tuple-element.112.refs_0_, bf16[1024,512]{1,0:T(8,128)(2,1)} %copy-done.9, bf16[1024,512]{1,0:T(8,128)(2,1)} %collective-permute-done.5.refs_2_, ...), custom_call_target="tpu_custom_call" | custom-call | flops 100000000 | bytes 20971520 | tf_op jit(solution)/shard_map/complete_blocks_2/pallas_call | solution.py:598
  451.6 46.2 %collective-permute-done.17.refs_3_.refs_4_ = bf16[2,1024,512]{2,1,0:T(8,128)(2,1)} collective-permute-done((bf16[2,1024,512]{2,1,0:T(8,128)(2,1)}, bf16[2,1024,512]{2,1,0:T(8,128)(2,1)}, u32[]{:S(2)}, u32[]{:S(2)}) %collective-permute-start.17) | collective-permute-done | bytes 2097184 | tf_op jit(solution)/shard_map/ppermute | solution.py:669
  497.8 93.5 %experts_b_own_0.1 = (f32[1024,512]{1,0:T(8,128)}, bf16[1024,512]{1,0:T(8,128)(2,1)}, bf16[1024,512]{1,0:T(8,128)(2,1)}, bf16[1024,512]{1,0:T(8,128)(2,1)}, f32[16,960,448]{2,1,0:T(8,128)}) custom-call(s32[20480]{0:T(1024)} %bitcast.61, s32[131072]{0:T(1024)} %bitcast.55, f32[1056,128]{1,0:T(8,128)} %get-tuple-element.102.refs_2_, ...), custom_call_target="tpu_custom_call" | custom-call | flops 18790481920 | bytes 13762560 | tf_op jit(solution)/shard_map/experts_b_own_0/pallas_call | solution.py:415
  591.9 3.5 collective-permute-done.18.refs_5_.refs_6_
  595.4 3.0 collective-permute-done.19.refs_9_.refs_10_
  598.4 76.5 %experts_b_other_0.1 = (bf16[2,32,320,448]{3,2,1,0:T(8,128)(2,1)}, bf16[2,32,320,448]{3,2,1,0:T(8,128)(2,1)}, bf16[2,32,320,448]{3,2,1,0:T(8,128)(2,1)}, bf16[16,3,320,448]{3,2,1,0:T(8,128)(2,1)}) custom-call(s32[20480]{0:T(1024)} %bitcast.62, s32[131072]{0:T(1024)} %bitcast.56, ...), custom_call_target="tpu_custom_call", output_to_operand_aliasing={{0}: (15, {}), {1}: (16, {}), {2}: (17, {})} | custom-call | flops 14092861440 | bytes 13762560 | tf_op jit(solution)/shard_map/experts_b_other_0/pallas_call | solution.py:415
  676.3 3.3 convolution_bitcast_fusion.1
  688.7 9.9 %collective-permute-done.20.tab_ref = s32[32]{0:T(128)S(1)} collective-permute-done((s32[32]{0:T(128)S(1)}, s32[32]{0:T(128)S(1)}, u32[]{:S(2)}, u32[]{:S(2)}) %collective-permute-start.20) | collective-permute-done | bytes 160 | tf_op jit(solution)/shard_map/ppermute | solution.py:669
  699.2 12.3 %place_1.1 = (bf16[2,32,320,448]{3,2,1,0:T(8,128)(2,1)}, bf16[2,32,320,448]{3,2,1,0:T(8,128)(2,1)}, bf16[2,32,320,448]{3,2,1,0:T(8,128)(2,1)}) custom-call(s32[32]{0:T(128)} %copy-done.17, bf16[16,3,320,448]{3,2,1,0:T(8,128)(2,1)} %collective-permute-done.16.got_ref, ...), custom_call_target="tpu_custom_call", output_to_operand_aliasing={{0}: (2, {}), {1}: (3, {}), {2}: (4, {})} | custom-call | bytes 27525120 | tf_op jit(solution)/shard_map/place_1/pallas_call | solution.py:445
  714.1 22.4 %total_grads.1 = bf16[2,448,448]{2,1,0:T(8,128)(2,1)} custom-call(f32[2,448,448]{2,1,0:T(8,128)} %pad_maximum_fusion.2.g_ref), custom_call_target="tpu_custom_call" | custom-call | flops 10000000 | bytes 3211264 | tf_op jit(solution)/shard_map/total_grads/pallas_call | solution.py:648
  736.5 12.4 %place_0.1 = (bf16[2,32,320,448]{3,2,1,0:T(8,128)(2,1)}, bf16[2,32,320,448]{3,2,1,0:T(8,128)(2,1)}, bf16[2,32,320,448]{3,2,1,0:T(8,128)(2,1)}) custom-call(s32[32]{0:T(128)} %copy-done.17, bf16[16,3,320,448]{3,2,1,0:T(8,128)(2,1)} %collective-permute-done.21.got_ref, ...), custom_call_target="tpu_custom_call", output_to_operand_aliasing={{0}: (2, {}), {1}: (3, {}), {2}: (4, {})} | custom-call | bytes 27525120 | tf_op jit(solution)/shard_map/place_0/pallas_call | solution.py:445
  (111 shorter events, 38.1 us)
Async XLA Ops:
  5.1 26.5 %collective-permute-start = (bf16[1024,512]{1,0:T(8,128)(2,1)}, bf16[1024,512]{1,0:T(8,128)(2,1)}, u32[]{:S(2)}, u32[]{:S(2)}) collective-permute-start(bf16[1024,512]{1,0:T(8,128)(2,1)} %get-tuple-element.207), channel_id=1, source_target_pairs={{0,4},{4,0},{1,5},{5,1},{2,6},{6,2},{3,7},{7,3}} | collective-permute-start | bytes 3145736 | tf_op jit(solution)/shard_map/ppermute | solution.py:669
  33.1 47.4 %copy-start = (bf16[2,1024,512]{2,1,0:T(8,128)(2,1)}, bf16[2,1024,512]{2,1,0:T(8,128)(2,1)S(1)}, u32[]{:S(2)}) copy-start(bf16[2,1024,512]{2,1,0:T(8,128)(2,1)S(1)} %pad_maximum_fusion.refs_3_.refs_4_) | copy-start | bytes 6291460
  33.1 47.4 %collective-permute-start.1 = (bf16[2,1024,512]{2,1,0:T(8,128)(2,1)S(1)}, bf16[2,1024,512]{2,1,0:T(8,128)(2,1)}, u32[]{:S(2)}, u32[]{:S(2)}) collective-permute-start(bf16[2,1024,512]{2,1,0:T(8,128)(2,1)S(1)} %pad_maximum_fusion.refs_3_.refs_4_), channel_id=1, source_target_pairs={{0,1},{1,0},{2,3},{3,2},{4,5},{5,4},{6,7},{7,6}} | collective-permute-start | bytes 6291464 | tf_op jit(solution)/shard_map/ppermute | solution.py:669
  52.0 25.7 %collective-permute-start.2 = (bf16[1024,512]{1,0:T(8,128)(2,1)}, bf16[1024,512]{1,0:T(8,128)(2,1)}, u32[]{:S(2)}, u32[]{:S(2)}) collective-permute-start(bf16[1024,512]{1,0:T(8,128)(2,1)} %pad.13), channel_id=1, source_target_pairs={{0,4},{4,0},{1,5},{5,1},{2,6},{6,2},{3,7},{7,3}} | collective-permute-start | bytes 3145736 | tf_op jit(solution)/shard_map/ppermute | solution.py:669
  201.3 47.8 %collective-permute-start.7 = (bf16[2,1024,512]{2,1,0:T(8,128)(2,1)}, bf16[2,1024,512]{2,1,0:T(8,128)(2,1)}, u32[]{:S(2)}, u32[]{:S(2)}) collective-permute-start(bf16[2,1024,512]{2,1,0:T(8,128)(2,1)} %pad_maximum_fusion.1.refs_7_.refs_8_), channel_id=1, source_target_pairs={{0,2},{2,0},{1,3},{3,1},{4,6},{6,4},{5,7},{7,5}} | collective-permute-start | bytes 6291464 | tf_op jit(solution)/shard_map/ppermute | solution.py:669
  201.7 47.5 %collective-permute-start.3 = (bf16[2,1024,512]{2,1,0:T(8,128)(2,1)}, bf16[2,1024,512]{2,1,0:T(8,128)(2,1)}, u32[]{:S(2)}, u32[]{:S(2)}) collective-permute-start(bf16[2,1024,512]{2,1,0:T(8,128)(2,1)} %pad_maximum_fusion.1.refs_7_.refs_8_), channel_id=1, source_target_pairs={{0,1},{1,0},{2,3},{3,2},{4,5},{5,4},{6,7},{7,6}} | collective-permute-start | bytes 6291464 | tf_op jit(solution)/shard_map/ppermute | solution.py:669
  249.2 97.8 %collective-permute-start.8 = (bf16[2,1024,512]{2,1,0:T(8,128)(2,1)}, bf16[2,1024,512]{2,1,0:T(8,128)(2,1)}, u32[]{:S(2)}, u32[]{:S(2)}) collective-permute-start(bf16[2,1024,512]{2,1,0:T(8,128)(2,1)} %collective-permute-done.7.refs_7_.refs_8_), channel_id=1, source_target_pairs={{0,1},{1,0},{2,3},{3,2},{4,5},{5,4},{6,7},{7,6}} | collective-permute-start | bytes 6291464 | tf_op jit(solution)/shard_map/ppermute | solution.py:669
  344.3 72.5 %collective-permute-start.4 = (bf16[1024,512]{1,0:T(8,128)(2,1)}, bf16[1024,512]{1,0:T(8,128)(2,1)S(1)}, u32[]{:S(2)}, u32[]{:S(2)}) collective-permute-start(bf16[1024,512]{1,0:T(8,128)(2,1)} %get-tuple-element.113), channel_id=1, source_target_pairs={{0,4},{4,0},{1,5},{5,1},{2,6},{6,2},{3,7},{7,3}} | collective-permute-start | bytes 3145736 | tf_op jit(solution)/shard_map/ppermute | solution.py:669
  346.8 70.1 %collective-permute-start.5 = (bf16[1024,512]{1,0:T(8,128)(2,1)}, bf16[1024,512]{1,0:T(8,128)(2,1)}, u32[]{:S(2)}, u32[]{:S(2)}) collective-permute-start(bf16[1024,512]{1,0:T(8,128)(2,1)} %get-tuple-element.114), channel_id=1, source_target_pairs={{0,1},{1,0},{2,3},{3,2},{4,5},{5,4},{6,7},{7,6}} | collective-permute-start | bytes 3145736 | tf_op jit(solution)/shard_map/ppermute | solution.py:669
  347.0 69.9 %collective-permute-start.6 = (bf16[1024,512]{1,0:T(8,128)(2,1)}, bf16[1024,512]{1,0:T(8,128)(2,1)}, u32[]{:S(2)}, u32[]{:S(2)}) collective-permute-start(bf16[1024,512]{1,0:T(8,128)(2,1)} %get-tuple-element.115), channel_id=1, source_target_pairs={{0,5},{1,4},{4,1},{5,0},{2,7},{3,6},{6,3},{7,2}} | collective-permute-start | bytes 3145736 | tf_op jit(solution)/shard_map/ppermute | solution.py:670
  448.9 226.0 %collective-permute-start.16 = (bf16[16,3,320,448]{3,2,1,0:T(8,128)(2,1)}, bf16[16,3,320,448]{3,2,1,0:T(8,128)(2,1)}, u32[]{:S(2)}, u32[]{:S(2)}) collective-permute-start(bf16[16,3,320,448]{3,2,1,0:T(8,128)(2,1)} %get-tuple-element.150), channel_id=1, source_target_pairs={{0,1},{1,0},{2,3},{3,2},{4,5},{5,4},{6,7},{7,6}} | collective-permute-start | bytes 41287688 | tf_op jit(solution)/shard_map/ppermute | solution.py:669
  449.3 48.5 %collective-permute-start.17 = (bf16[2,1024,512]{2,1,0:T(8,128)(2,1)}, bf16[2,1024,512]{2,1,0:T(8,128)(2,1)}, u32[]{:S(2)}, u32[]{:S(2)}) collective-permute-start(bf16[2,1024,512]{2,1,0:T(8,128)(2,1)} %copy-done), channel_id=1, source_target_pairs={{0,2},{2,0},{1,3},{3,1},{4,6},{6,4},{5,7},{7,5}} | collective-permute-start | bytes 6291464 | tf_op jit(solution)/shard_map/ppermute | solution.py:669
  449.5 141.8 %collective-permute-start.9 = (bf16[2,1024,512]{2,1,0:T(8,128)(2,1)}, bf16[2,1024,512]{2,1,0:T(8,128)(2,1)}, u32[]{:S(2)}, u32[]{:S(2)}) collective-permute-start(bf16[2,1024,512]{2,1,0:T(8,128)(2,1)} %get-tuple-element.133.refs_7_.refs_8_), channel_id=1, source_target_pairs={{0,2},{2,0},{1,3},{3,1},{4,6},{6,4},{5,7},{7,5}} | collective-permute-start | bytes 6291464 | tf_op jit(solution)/shard_map/ppermute | solution.py:669
  451.3 140.0 %collective-permute-start.10 = (bf16[1024,512]{1,0:T(8,128)(2,1)}, bf16[1024,512]{1,0:T(8,128)(2,1)S(1)}, u32[]{:S(2)}, u32[]{:S(2)}) collective-permute-start(bf16[1024,512]{1,0:T(8,128)(2,1)} %get-tuple-element.134), channel_id=1, source_target_pairs={{0,4},{4,0},{1,5},{5,1},{2,6},{6,2},{3,7},{7,3}} | collective-permute-start | bytes 3145736 | tf_op jit(solution)/shard_map/ppermute | solution.py:669
  451.6 139.7 %collective-permute-start.11 = (bf16[1024,512]{1,0:T(8,128)(2,1)}, bf16[1024,512]{1,0:T(8,128)(2,1)}, u32[]{:S(2)}, u32[]{:S(2)}) collective-permute-start(bf16[1024,512]{1,0:T(8,128)(2,1)} %get-tuple-element.135), channel_id=1, source_target_pairs={{0,1},{1,0},{2,3},{3,2},{4,5},{5,4},{6,7},{7,6}} | collective-permute-start | bytes 3145736 | tf_op jit(solution)/shard_map/ppermute | solution.py:669
  497.8 93.6 %collective-permute-start.12 = (bf16[1024,512]{1,0:T(8,128)(2,1)}, bf16[1024,512]{1,0:T(8,128)(2,1)}, u32[]{:S(2)}, u32[]{:S(2)}) collective-permute-start(bf16[1024,512]{1,0:T(8,128)(2,1)} %get-tuple-element.136), channel_id=1, source_target_pairs={{0,5},{1,4},{4,1},{5,0},{2,7},{3,6},{6,3},{7,2}} | collective-permute-start | bytes 3145736 | tf_op jit(solution)/shard_map/ppermute | solution.py:670
  591.3 83.6 %copy-start.7 = (bf16[1024,512]{1,0:T(8,128)(2,1)}, bf16[1024,512]{1,0:T(8,128)(2,1)S(1)}, u32[]{:S(2)}) copy-start(bf16[1024,512]{1,0:T(8,128)(2,1)S(1)} %collective-permute-done.10) | copy-start | bytes 3145732
  591.3 4.1 collective-permute-start.18
  591.4 7.1 collective-permute-start.19
  591.9 83.0 %collective-permute-start.13 = (bf16[1024,512]{1,0:T(8,128)(2,1)}, bf16[1024,512]{1,0:T(8,128)(2,1)}, u32[]{:S(2)}, u32[]{:S(2)}) collective-permute-start(bf16[1024,512]{1,0:T(8,128)(2,1)} %get-tuple-element.147), channel_id=1, source_target_pairs={{0,4},{4,0},{1,5},{5,1},{2,6},{6,2},{3,7},{7,3}} | collective-permute-start | bytes 3145736 | tf_op jit(solution)/shard_map/ppermute | solution.py:669
  591.9 83.1 %collective-permute-start.14 = (bf16[1024,512]{1,0:T(8,128)(2,1)}, bf16[1024,512]{1,0:T(8,128)(2,1)}, u32[]{:S(2)}, u32[]{:S(2)}) collective-permute-start(bf16[1024,512]{1,0:T(8,128)(2,1)} %get-tuple-element.148), channel_id=1, source_target_pairs={{0,1},{1,0},{2,3},{3,2},{4,5},{5,4},{6,7},{7,6}} | collective-permute-start | bytes 3145736 | tf_op jit(solution)/shard_map/ppermute | solution.py:669
  595.4 79.5 %collective-permute-start.15 = (bf16[1024,512]{1,0:T(8,128)(2,1)}, bf16[1024,512]{1,0:T(8,128)(2,1)}, u32[]{:S(2)}, u32[]{:S(2)}) collective-permute-start(bf16[1024,512]{1,0:T(8,128)(2,1)} %get-tuple-element.149), channel_id=1, source_target_pairs={{0,5},{1,4},{4,1},{5,0},{2,7},{3,6},{6,3},{7,2}} | collective-permute-start | bytes 3145736 | tf_op jit(solution)/shard_map/ppermute | solution.py:670
  675.0 61.5 %collective-permute-start.21 = (bf16[16,3,320,448]{3,2,1,0:T(8,128)(2,1)}, bf16[16,3,320,448]{3,2,1,0:T(8,128)(2,1)}, u32[]{:S(2)}, u32[]{:S(2)}) collective-permute-start(bf16[16,3,320,448]{3,2,1,0:T(8,128)(2,1)} %get-tuple-element.171), channel_id=1, source_target_pairs={{0,1},{1,0},{2,3},{3,2},{4,5},{5,4},{6,7},{7,6}} | collective-permute-start | bytes 41287688 | tf_op jit(solution)/shard_map/ppermute | solution.py:669
  675.8 22.9 %collective-permute-start.20 = (s32[32]{0:T(128)S(1)}, s32[32]{0:T(128)S(1)}, u32[]{:S(2)}, u32[]{:S(2)}) collective-permute-start(s32[32]{0:T(128)S(1)} %pad_add_fusion), channel_id=1, source_target_pairs={{0,1},{1,0},{2,3},{3,2},{4,5},{5,4},{6,7},{7,6}} | collective-permute-start | bytes 392 | tf_op jit(solution)/shard_map/ppermute | solution.py:669
  (16 other events, 132.2 us)
